TPU v7x, 32 devices: a 4x4x1 block of a 4x4x8 slice. The times are simulated.
32 devices in a mesh: dp: 1 (over z), tp: 4 (over y), sq: 8 (over x, core).
Axes of the slice: x: 4, y: 4, z: 1, core: 2. Of those that a mesh axis runs over, the one named last changes fastest.
The devices are a block of a 4x4x8 slice.
Arguments:
- x_steps: bfloat16 [4, 32, 6144], P(None, 'dp')
- positions: int32 [32], P('dp')
- k_cache: bfloat16 [32, 4096, 4, 128], P('dp', 'sq', 'tp')
- v_cache: bfloat16 [32, 4096, 4, 128], P('dp', 'sq', 'tp')
- w_q: bfloat16 [6144, 6144], P(None, 'tp')
- b_q: bfloat16 [6144], P('tp')
- w_k: bfloat16 [6144, 512], P(None, 'tp')
- b_k: bfloat16 [512], P('tp')
- w_v: bfloat16 [6144, 512], P(None, 'tp')
- b_v: bfloat16 [512], P('tp')
- w_o: bfloat16 [6144, 6144], P('tp')
- b_o: bfloat16 [6144], replicated
- ln1_gain: bfloat16 [6144], replicated
- ln1_bias: bfloat16 [6144], replicated
- ln2_gain: bfloat16 [6144], replicated
- ln2_bias: bfloat16 [6144], replicated
- w_fc: bfloat16 [6144, 24576], P(None, 'tp')
- b_fc: bfloat16 [24576], P('tp')
- w_proj: bfloat16 [24576, 6144], P('tp')
- b_proj: bfloat16 [6144], replicated
Outputs:
- output 1: bfloat16 [4, 32, 6144], P(None, 'dp')
- output 2: bfloat16 [32, 4096, 4, 128], P('dp', 'sq', 'tp')
- output 3: bfloat16 [32, 4096, 4, 128], P('dp', 'sq', 'tp')
All inputs are finite; a program needn't handle non-finite values.
Results may differ from a plain program's by a relative error of at most 0.0152474.
Values sent between devices are 32-bit elements.
A program may use at most 768 MiB of HBM per device.

v0:
```python
import jax
import jax.numpy as jnp
from jax import lax
from jax.sharding import PartitionSpec as P

ROPE_BASE = 1000000.0
LN_EPS = 1e-5
NEG_BIG = -1e30


def layer_norm(vectors, gain, shift):
    row_mean = jnp.mean(vectors, axis=-1, keepdims=True)
    centered = vectors - row_mean
    row_var = jnp.mean(centered * centered, axis=-1, keepdims=True)
    return centered * lax.rsqrt(row_var + LN_EPS) * gain.astype(jnp.float32) + shift.astype(jnp.float32)


def rope_tables(positions, head_dim):
    half_dim = head_dim // 2
    inv_freq = jnp.power(jnp.float32(ROPE_BASE), -2.0 * jnp.arange(half_dim, dtype=jnp.float32) / head_dim)
    angle = positions.astype(jnp.float32)[..., None] * inv_freq
    return jnp.cos(angle), jnp.sin(angle)


def apply_rope(vectors, cos_t, sin_t):
    half_dim = vectors.shape[-1] // 2
    first = vectors[..., :half_dim]
    second = vectors[..., half_dim:]
    return jnp.concatenate([first * cos_t - second * sin_t, second * cos_t + first * sin_t], axis=-1)


def linear(rows_in, weight, bias):
    return jnp.dot(rows_in, weight, preferred_element_type=jnp.float32) + bias.astype(jnp.float32)


def new_entries(x_in, cur_pos, ln1_gain, ln1_bias, w_q, b_q, w_k, b_k, w_v, b_v, kv_count, head_dim):
    batch = x_in.shape[0]
    group = w_q.shape[1] // (kv_count * head_dim)
    hidden = layer_norm(x_in.astype(jnp.float32), ln1_gain, ln1_bias).astype(jnp.bfloat16)
    query = linear(hidden, w_q, b_q).astype(jnp.bfloat16)
    key_new = linear(hidden, w_k, b_k).astype(jnp.bfloat16)
    val_new = linear(hidden, w_v, b_v).astype(jnp.bfloat16)
    cos_t, sin_t = rope_tables(cur_pos, head_dim)
    q_rot = apply_rope(query.reshape(batch, kv_count, group, head_dim).astype(jnp.float32), cos_t[:, None, None, :], sin_t[:, None, None, :]).astype(jnp.bfloat16)
    k_rot = apply_rope(key_new.reshape(batch, kv_count, head_dim).astype(jnp.float32), cos_t[:, None, :], sin_t[:, None, :]).astype(jnp.bfloat16)
    return q_rot, k_rot, val_new.reshape(batch, kv_count, head_dim)


def partial_attention(q_rot, key_buf, val_buf, slot_ok, head_dim):
    slot_mask = slot_ok[:, None, None, :]
    scores = jnp.einsum("bgrd,bwgd->bgrw", q_rot, key_buf, preferred_element_type=jnp.float32) * head_dim ** -0.5
    scores = jnp.where(slot_mask, scores, NEG_BIG)
    part_max = jnp.max(scores, axis=-1)
    weights = jnp.where(slot_mask, jnp.exp(scores - part_max[..., None]), 0.0)
    part_sum = jnp.sum(weights, axis=-1)
    part_out = jnp.einsum("bgrw,bwgd->bgrd", weights.astype(jnp.bfloat16), val_buf, preferred_element_type=jnp.float32)
    return part_max, part_sum, part_out


def layer_tail(x_in, attn_out, w_o, b_o, ln2_gain, ln2_bias, w_fc, b_fc, w_proj, b_proj):
    attn_proj = lax.psum(jnp.dot(attn_out, w_o, preferred_element_type=jnp.float32), "tp")
    x_mid = (x_in.astype(jnp.float32) + attn_proj + b_o.astype(jnp.float32)).astype(jnp.bfloat16)
    hidden = layer_norm(x_mid.astype(jnp.float32), ln2_gain, ln2_bias).astype(jnp.bfloat16)
    gelu_out = jax.nn.gelu(linear(hidden, w_fc, b_fc), approximate=True).astype(jnp.bfloat16)
    mlp_out = lax.psum(jnp.dot(gelu_out, w_proj, preferred_element_type=jnp.float32), "tp")
    return (x_mid.astype(jnp.float32) + mlp_out + b_proj.astype(jnp.float32)).astype(jnp.bfloat16)


def solution(mesh):
    sq_size = mesh.shape["sq"]
    act_spec = P(None, "dp", None)
    cache_spec = P("dp", "sq", "tp", None)
    col_spec = P(None, "tp")
    row_spec = P("tp", None)
    vec_spec = P("tp")
    rep_spec = P(None)
    in_specs = (act_spec, P("dp"), cache_spec, cache_spec, col_spec, vec_spec, col_spec, vec_spec,
                col_spec, vec_spec, row_spec, rep_spec, rep_spec, rep_spec, rep_spec, rep_spec,
                col_spec, vec_spec, row_spec, rep_spec)
    out_specs = (act_spec, cache_spec, cache_spec)

    def per_device(x_steps, positions, key_buf, val_buf, w_q, b_q, w_k, b_k, w_v, b_v, w_o, b_o,
                   ln1_gain, ln1_bias, ln2_gain, ln2_bias, w_fc, b_fc, w_proj, b_proj):
        steps, batch = x_steps.shape[0], x_steps.shape[1]
        slots_local, kv_local, head_dim = key_buf.shape[1], key_buf.shape[2], key_buf.shape[3]
        slots = slots_local * sq_size
        first_slot = lax.axis_index("sq") * slots_local
        slot_ids = first_slot + jnp.arange(slots_local, dtype=jnp.int32)
        batch_ids = jnp.arange(batch, dtype=jnp.int32)
        outputs = []
        for step_idx in range(steps):
            x_in = x_steps[step_idx]
            cur_pos = positions + step_idx
            q_rot, k_rot, v_heads = new_entries(x_in, cur_pos, ln1_gain, ln1_bias, w_q, b_q, w_k, b_k, w_v, b_v, kv_local, head_dim)
            local_slot = cur_pos % slots - first_slot
            local_slot = jnp.where((local_slot >= 0) & (local_slot < slots_local), local_slot, slots_local)
            key_buf = key_buf.at[batch_ids, local_slot].set(k_rot, mode="drop")
            val_buf = val_buf.at[batch_ids, local_slot].set(v_heads, mode="drop")
            held_pos = cur_pos[:, None] - (cur_pos[:, None] - slot_ids[None, :]) % slots
            part_max, part_sum, part_out = partial_attention(q_rot, key_buf, val_buf, held_pos >= 0, head_dim)
            stats = jnp.concatenate([part_out, part_sum[..., None], part_max[..., None]], axis=-1)
            gathered = lax.all_gather(stats, "sq")
            all_max = gathered[..., head_dim + 1]
            glob_max = jnp.max(all_max, axis=0)
            rescale = jnp.exp(all_max - glob_max)
            total_sum = jnp.sum(rescale * gathered[..., head_dim], axis=0)
            total_out = jnp.sum(rescale[..., None] * gathered[..., :head_dim], axis=0)
            attn_out = (total_out / total_sum[..., None]).astype(jnp.bfloat16).reshape(batch, -1)
            outputs.append(layer_tail(x_in, attn_out, w_o, b_o, ln2_gain, ln2_bias, w_fc, b_fc, w_proj, b_proj))
        return jnp.stack(outputs), key_buf, val_buf

    return jax.shard_map(per_device, mesh=mesh, in_specs=in_specs, out_specs=out_specs, check_vma=False)
```

profile of v0, /device:TPU:97, one launch (start us, length us, event | category | flops | bytes accessed | tf_op | source)
XLA Modules:
  0.0 588.9 jit_solution(15814464945443852638)
XLA Ops:
  7.3 4.8 copy.217
  16.5 10.5 %fusion.1 = f32[32,1536]{1,0:T(8,128)} fusion(bf16[6144,1536]{1,0:T(8,128)(2,1)} %param.24, f32[1536]{0:T(1024)S(1)} %convert_element_type.401, f32[6144]{0:T(1024)S(1)} %convert_element_type.399, f32[6144]{0:T(1024)S(1)} %convert_element_type.398, f32[32]{0:T(128)S(1)} %add_rsqrt_fusion.7, f32[32]{0:T(128)S(1)} %get-tuple-element.109, ...), kind=kOutput, calls=%fused_computation.17 | convolution fusion | flops 605306880 | bytes 19522560 | tf_op jit(solution)/shard_map/dot_general | solution.py:33
  30.4 4.4 scatter_fusion
  54.2 10.5 %fusion.3 = f32[32,1536]{1,0:T(8,128)} fusion(bf16[6144,1536]{1,0:T(8,128)(2,1)} %param.24, f32[1536]{0:T(1024)S(1)} %convert_element_type.401, f32[32]{0:T(128)S(1)} %add_rsqrt_fusion.5, f32[32]{0:T(128)S(1)} %copy-done.38, f32[6144]{0:T(1024)S(1)} %convert_element_type.399, f32[6144]{0:T(1024)S(1)} %convert_element_type.398, ...), kind=kOutput, calls=%fused_computation.19 | convolution fusion | flops 605306880 | bytes 19522560 | tf_op jit(solution)/shard_map/dot_general | solution.py:33
  69.8 4.4 scatter_fusion.2
  76.0 4.4 scatter_fusion.3
  90.5 9.4 %fusion.5 = f32[32,1536]{1,0:T(8,128)S(1)} fusion(bf16[6144,1536]{1,0:T(8,128)(2,1)} %param.24, f32[1536]{0:T(1024)S(1)} %convert_element_type.401, f32[32]{0:T(128)} %add_rsqrt_fusion.3, f32[32]{0:T(128)} %copy-done.35, f32[6144]{0:T(1024)S(1)} %convert_element_type.399, f32[6144]{0:T(1024)S(1)} %convert_element_type.398, ...), kind=kOutput, calls=%fused_computation.21 | convolution fusion | flops 605306880 | bytes 19521792 | tf_op jit(solution)/shard_map/dot_general | solution.py:33
  100.0 4.4 scatter_fusion.4
  106.3 4.4 scatter_fusion.5
  119.9 8.2 %fusion.7 = f32[32,1536]{1,0:T(8,128)S(1)} fusion(bf16[6144,1536]{1,0:T(8,128)(2,1)} %param.24, f32[1536]{0:T(1024)S(1)} %convert_element_type.401, f32[32]{0:T(128)S(1)} %copy-done.49, f32[32]{0:T(128)S(1)} %copy-done.34, f32[6144]{0:T(1024)S(1)} %convert_element_type.399, f32[6144]{0:T(1024)S(1)} %convert_element_type.398, ...), kind=kOutput, calls=%fused_computation.23 | convolution fusion | flops 605306880 | bytes 19522560 | tf_op jit(solution)/shard_map/dot_general | solution.py:33
  128.2 4.4 scatter_fusion.6
  134.4 4.4 scatter_fusion.7
  168.4 10.2 %all-gather.15.cloned.1.call-done = f32[256,1,12,130]{3,1,2,0:T(1,128)} async-done(((f32[32,1,12,130]{3,1,2,0:T(1,128)}), f32[256,1,12,130]{3,1,2,0:T(1,128)}) %all-gather.15.cloned.1.call-update) | async-done | bytes 1597456 | tf_op jit(solution)/shard_map/all_gather | solution.py:102
  184.7 10.8 %fusion.257 = f32[32,6144]{1,0:T(8,128)} fusion(bf16[1536,6144]{1,0:T(8,128)(2,1)} %param.30, f32[32,12,128]{2,0,1:T(8,128)S(1)} %fusion.11, f32[32,12]{0,1:T(8,128)S(1)} %fusion.282), kind=kOutput, calls=%fused_computation.338 | convolution fusion | flops 604078080 | bytes 19858944 | tf_op jit(solution)/shard_map/dot_general | solution.py:61
  209.4 69.5 %all-reduce.7.cloned.1.call-done = (f32[32,6144]{1,0:T(8,128)}, f32[32,6144]{1,0:T(8,128)}, f32[32,6144]{1,0:T(8,128)}, f32[32,6144]{1,0:T(8,128)}) async-done(((f32[32,6144]{1,0:T(8,128)}, f32[32,6144]{1,0:T(8,128)}, f32[32,6144]{1,0:T(8,128)}, f32[32,6144]{1,0:T(8,128)}), (f32[32,6144]{1,0:T(8,128)}, f32[32,6144]{1,0:T(8,128)}, f32[32,6144]{1,0:T(8,128)}, ...) | async-done | bytes 3145744 | tf_op jit(solution)/shard_map/psum | solution.py:61
  283.1 27.6 %fusion.113.clone.4 = bf16[32,6144]{1,0:T(8,128)(2,1)S(1)} fusion(bf16[6144,6144]{1,0:T(8,128)(2,1)} %param.36, bf16[32,6144]{1,0:T(8,128)(2,1)S(1)} %get-tuple-element.32, f32[6144]{0:T(1024)S(1)} %convert_element_type.421, f32[6144]{0:T(1024)S(1)} %convert_element_type.419, f32[6144]{0:T(1024)S(1)} %convert_element_type.418, ...), kind=kOutput, calls=%fused_computation.194.clone.clone.clone.1 | convolution fusion | flops 2419064832 | bytes 76357888 | tf_op jit(solution)/shard_map/dot_general | solution.py:33
  310.7 27.7 %fusion.124.clone.4 = bf16[32,6144]{1,0:T(8,128)(2,1)S(1)} fusion(bf16[6144,6144]{1,0:T(8,128)(2,1)} %param.36, bf16[32,6144]{1,0:T(8,128)(2,1)S(1)} %get-tuple-element.40, f32[32]{0:T(128)S(1)} %add_rsqrt_fusion.4, f32[32]{0:T(128)S(1)} %broadcast_multiply_fusion.4, f32[6144]{0:T(1024)} %copy-done.16, f32[6144]{0:T(1024)} %copy-done.14, ...), kind=kOutput, calls=%fused_computation.205.clone.clone.clone.1 | convolution fusion | flops 2419064832 | bytes 76357888 | tf_op jit(solution)/shard_map/dot_general | solution.py:33
  338.4 28.2 %fusion.114 = f32[32,6144]{1,0:T(8,128)} fusion(bf16[6144,6144]{1,0:T(8,128)(2,1)} %param.38, bf16[32,6144]{1,0:T(8,128)(2,1)S(1)} %fusion.113.clone.4), kind=kOutput, calls=%fused_computation.195 | convolution fusion | flops 2415919104 | bytes 76677120 | tf_op jit(solution)/shard_map/dot_general | solution.py:65
  366.6 28.4 %fusion.125 = f32[32,6144]{1,0:T(8,128)} fusion(bf16[6144,6144]{1,0:T(8,128)(2,1)} %param.38, bf16[32,6144]{1,0:T(8,128)(2,1)S(1)} %fusion.124.clone.4), kind=kOutput, calls=%fused_computation.206 | convolution fusion | flops 2415919104 | bytes 76677120 | tf_op jit(solution)/shard_map/dot_general | solution.py:65
  395.3 27.6 %fusion.135.clone.2 = bf16[32,6144]{1,0:T(8,128)(2,1)S(1)} fusion(bf16[6144,6144]{1,0:T(8,128)(2,1)} %param.36, bf16[32,6144]{1,0:T(8,128)(2,1)S(1)} %get-tuple-element.42, f32[32]{0:T(128)S(1)} %add_rsqrt_fusion.2, f32[32]{0:T(128)S(1)} %broadcast_multiply_fusion.2, f32[6144]{0:T(1024)S(1)} %copy-done.17, f32[6144]{0:T(1024)S(1)} %copy-done.15, ...), kind=kOutput, calls=%fused_computation.216.clone.clone.clone | convolution fusion | flops 2419064832 | bytes 76357888 | tf_op jit(solution)/shard_map/dot_general | solution.py:33
  422.9 28.2 %fusion.136 = f32[32,6144]{1,0:T(8,128)} fusion(bf16[6144,6144]{1,0:T(8,128)(2,1)} %param.38, bf16[32,6144]{1,0:T(8,128)(2,1)S(1)} %fusion.135.clone.2), kind=kOutput, calls=%fused_computation.217 | convolution fusion | flops 2415919104 | bytes 76677120 | tf_op jit(solution)/shard_map/dot_general | solution.py:65
  451.4 27.8 %fusion.146.clone.2 = bf16[32,6144]{1,0:T(8,128)(2,1)S(1)} fusion(bf16[6144,6144]{1,0:T(8,128)(2,1)} %param.36, bf16[32,6144]{1,0:T(8,128)(2,1)S(1)} %copy-done.10, f32[32]{0:T(128)S(1)} %add_rsqrt_fusion, f32[32]{0:T(128)S(1)} %broadcast_multiply_fusion, f32[6144]{0:T(1024)S(1)} %copy-done.17, f32[6144]{0:T(1024)S(1)} %copy-done.15, ...), kind=kOutput, calls=%fused_computation.227.clone.clone.clone | convolution fusion | flops 2419064832 | bytes 76357888 | tf_op jit(solution)/shard_map/dot_general | solution.py:33
  479.2 28.2 %fusion.147 = f32[32,6144]{1,0:T(8,128)} fusion(bf16[6144,6144]{1,0:T(8,128)(2,1)} %param.38, bf16[32,6144]{1,0:T(8,128)(2,1)S(1)} %fusion.146.clone.2), kind=kOutput, calls=%fused_computation.228 | convolution fusion | flops 2415919104 | bytes 76677120 | tf_op jit(solution)/shard_map/dot_general | solution.py:65
  508.7 69.2 %all-reduce.5.cloned.1.call-done = (f32[32,6144]{1,0:T(8,128)}, f32[32,6144]{1,0:T(8,128)}, f32[32,6144]{1,0:T(8,128)}, f32[32,6144]{1,0:T(8,128)}) async-done(((f32[32,6144]{1,0:T(8,128)}, f32[32,6144]{1,0:T(8,128)}, f32[32,6144]{1,0:T(8,128)}, f32[32,6144]{1,0:T(8,128)}), (f32[32,6144]{1,0:T(8,128)}, f32[32,6144]{1,0:T(8,128)}, f32[32,6144]{1,0:T(8,128)}, ...) | async-done | bytes 3145744 | tf_op jit(solution)/shard_map/psum | solution.py:65
  (266 shorter events, 115.7 us)
Async XLA Ops:
  7.2 140.9 %all-gather.9.cloned.1.call-start = ((), (), s32[]{:S(2)}) async-start(), calls=%async_computation | async-start | bytes 3538944 | tf_op jit(solution)/shard_map/all_gather | solution.py:102
  14.1 25.2 %copy-start.39 = (f32[64]{0:T(128)}, f32[64]{0:T(128)S(1)}, u32[]{:S(2)}) copy-start(f32[64]{0:T(128)S(1)} %multiply_power_fusion) | copy-start | bytes 772
  14.7 24.5 %copy-start.41 = (f32[32]{0:T(128)}, f32[32]{0:T(128)S(1)}, u32[]{:S(2)}) copy-start(f32[32]{0:T(128)S(1)} %get-tuple-element.84) | copy-start | bytes 388
  14.8 24.5 %copy-start.43 = (f32[32]{0:T(128)}, f32[32]{0:T(128)S(1)}, u32[]{:S(2)}) copy-start(f32[32]{0:T(128)S(1)} %get-tuple-element.85) | copy-start | bytes 388
  14.8 24.5 %copy-start.45 = (f32[32]{0:T(128)}, f32[32]{0:T(128)S(1)}, u32[]{:S(2)}) copy-start(f32[32]{0:T(128)S(1)} %get-tuple-element.86) | copy-start | bytes 388
  15.2 51.5 %copy-start.33 = (f32[32]{0:T(128)}, f32[32]{0:T(128)S(1)}, u32[]{:S(2)}) copy-start(f32[32]{0:T(128)S(1)} %get-tuple-element.106) | copy-start | bytes 388
  15.2 52.6 %copy-start.35 = (f32[32]{0:T(128)}, f32[32]{0:T(128)S(1)}, u32[]{:S(2)}) copy-start(f32[32]{0:T(128)S(1)} %get-tuple-element.107) | copy-start | bytes 388
  51.9 100.4 %all-gather.11.cloned.1.call-start = ((), (), s32[]{:S(2)}) async-start(), calls=%async_computation.1 | async-start | bytes 3538944 | tf_op jit(solution)/shard_map/all_gather | solution.py:102
  90.2 66.3 %all-gather.13.cloned.1.call-start = ((), (), s32[]{:S(2)}) async-start(), calls=%async_computation.2 | async-start | bytes 3538944 | tf_op jit(solution)/shard_map/all_gather | solution.py:102
  119.8 58.9 %all-gather.15.cloned.1.call-start = ((), (), s32[]{:S(2)}) async-start(), calls=%async_computation.3 | async-start | bytes 3538944 | tf_op jit(solution)/shard_map/all_gather | solution.py:102
  147.8 131.0 %all-reduce.7.cloned.1.call-start = ((), (), s32[]{:S(2)}) async-start(), calls=%async_computation.5 | async-start | bytes 6291456 | tf_op jit(solution)/shard_map/psum | solution.py:61
  208.7 369.2 %all-reduce.5.cloned.1.call-start = ((), (), s32[]{:S(2)}) async-start(), calls=%async_computation.4 | async-start | bytes 6291456 | tf_op jit(solution)/shard_map/psum | solution.py:65
  209.3 73.8 %copy-start.12 = (f32[6144]{0:T(1024)}, f32[6144]{0:T(1024)S(1)}, u32[]{:S(2)}) copy-start(f32[6144]{0:T(1024)S(1)} %convert_element_type.418) | copy-start | bytes 73732
  209.3 73.8 %copy-start.14 = (f32[6144]{0:T(1024)}, f32[6144]{0:T(1024)S(1)}, u32[]{:S(2)}) copy-start(f32[6144]{0:T(1024)S(1)} %convert_element_type.419) | copy-start | bytes 73732
  209.4 73.8 %copy-start.16 = (f32[6144]{0:T(1024)}, f32[6144]{0:T(1024)S(1)}, u32[]{:S(2)}) copy-start(f32[6144]{0:T(1024)S(1)} %convert_element_type.421) | copy-start | bytes 73732
  282.5 28.2 %copy-start.6 = (bf16[32,6144]{1,0:T(8,128)(2,1)}, bf16[32,6144]{1,0:T(8,128)(2,1)S(1)}, u32[]{:S(2)}) copy-start(bf16[32,6144]{1,0:T(8,128)(2,1)S(1)} %get-tuple-element.32) | copy-start | bytes 1179652
  282.5 28.2 %copy-start.8 = (bf16[32,6144]{1,0:T(8,128)(2,1)}, bf16[32,6144]{1,0:T(8,128)(2,1)S(1)}, u32[]{:S(2)}) copy-start(bf16[32,6144]{1,0:T(8,128)(2,1)S(1)} %get-tuple-element.40) | copy-start | bytes 1179652
  366.6 28.7 %copy-start.13 = (f32[6144]{0:T(1024)S(1)}, f32[6144]{0:T(1024)}, u32[]{:S(2)}) copy-start(f32[6144]{0:T(1024)} %copy-done.12) | copy-start | bytes 73732
  366.6 28.7 %copy-start.15 = (f32[6144]{0:T(1024)S(1)}, f32[6144]{0:T(1024)}, u32[]{:S(2)}) copy-start(f32[6144]{0:T(1024)} %copy-done.14) | copy-start | bytes 73732
  366.6 28.7 %copy-start.17 = (f32[6144]{0:T(1024)S(1)}, f32[6144]{0:T(1024)}, u32[]{:S(2)}) copy-start(f32[6144]{0:T(1024)} %copy-done.16) | copy-start | bytes 73732
  422.9 28.2 %copy-start.55 = (f32[32]{0:T(128)S(1)}, f32[32]{0:T(128)}, u32[]{:S(2)}) copy-start(f32[32]{0:T(128)} %get-tuple-element.43) | copy-start | bytes 388
  422.9 28.2 %copy-start.10 = (bf16[32,6144]{1,0:T(8,128)(2,1)S(1)}, bf16[32,6144]{1,0:T(8,128)(2,1)}, u32[]{:S(2)}) copy-start(bf16[32,6144]{1,0:T(8,128)(2,1)} %get-tuple-element.44) | copy-start | bytes 1179652
  507.3 70.6 %copy-start.7 = (bf16[32,6144]{1,0:T(8,128)(2,1)S(1)}, bf16[32,6144]{1,0:T(8,128)(2,1)}, u32[]{:S(2)}) copy-start(bf16[32,6144]{1,0:T(8,128)(2,1)} %copy-done.6) | copy-start | bytes 1179652
  507.3 70.6 %copy-start.9 = (bf16[32,6144]{1,0:T(8,128)(2,1)S(1)}, bf16[32,6144]{1,0:T(8,128)(2,1)}, u32[]{:S(2)}) copy-start(bf16[32,6144]{1,0:T(8,128)(2,1)} %copy-done.8) | copy-start | bytes 1179652
  (50 other events, 399.6 us)
Sparse Core Ops, SparseCore 0:
  52.0 29.4 all-gather.8
  90.3 29.8 all-gather.10
  121.8 28.2 all-gather.12
  152.2 26.4 all-gather.14
  208.8 70.0 all-reduce.6
  507.5 70.3 all-reduce.4
where the time goes:
time: 597 us; the launch traced here: 589 us
  matrix products  320 us (54%)
  waiting for transfers between devices  149 us (25%)
  local copies, waits for them, and re-layouts  68.3 us (11%)
  other arithmetic  34 us (6%)
  between operations  15.7 us (3%)
    dot_general x16, matrix products, linear(): jnp.dot(rows_in, weight, preferred_element_type=jnp.float32)  159 us
    dot_general x4, matrix products, layer_tail(): jnp.dot(gelu_out, w_proj, preferred_element_type=jnp.float32)  113 us
    psum x1, waiting for transfers between devices, layer_tail(): lax.psum(jnp.dot(attn_out, w_o, preferred_element_type=jnp.float32), 'tp')  69.5 us
    psum x1, waiting for transfers between devices, layer_tail(): lax.psum(jnp.dot(gelu_out, w_proj, preferred_element_type=jnp.float32), '...  69.2 us
    dot_general x4, matrix products, layer_tail(): jnp.dot(attn_out, w_o, preferred_element_type=jnp.float32)  23.8 us
    scatter x4, local copies, waits for them, and re-layouts, per_device(): val_buf = val_buf.at[batch_ids, local_slot].set(v_heads, mode='drop')  17.7 us
    scatter x4, local copies, waits for them, and re-layouts, per_device(): key_buf = key_buf.at[batch_ids, local_slot].set(k_rot, mode='drop')  17.7 us
    dot_general x4, matrix products, partial_attention(): jnp.einsum('bgrd,bwgd->bgrw', q_rot, key_buf, preferred_element_type=jnp....  14.2 us
  transfers between devices with their start and end apart: 6, of which 3 were waited for; matrix products, arithmetic and copies ran while one was open for 19% of the time, Pallas kernels for 0%

commit v1 on v0

v1 whole, which is shorter than its diff:
```python
import functools

import jax
import jax.numpy as jnp
from jax import lax
from jax.experimental import pallas as pl
from jax.experimental.pallas import tpu as pltpu
from jax.sharding import PartitionSpec as P

ROPE_BASE = 1000000.0
LN_EPS = 1e-5
NEG_BIG = -1e30
MESH = pl.DeviceIdType.MESH
F32 = jnp.float32
BF16 = jnp.bfloat16
VMEM_BYTES = 67043328


def one_hot_rows(size, inner):
    outer = size // inner
    row = lax.broadcasted_iota(jnp.int32, (size, size), 0)
    col = lax.broadcasted_iota(jnp.int32, (size, size), 1)
    source = lax.rem(row, outer) * inner + lax.div(row, outer)
    return jnp.where(col == source, 1.0, 0.0).astype(BF16)


def qkv_kernel(x_any, wq_any, wk_any, wv_any, bias_ref, vec_ref, cos_ref, sin_ref, out_ref,
               x_buf, w_buf, hid, x_sem, w_sem, *, batch, tiles, tile, head_dim):
    rows, width = x_buf.shape
    x_copy = pltpu.make_async_copy(x_any, x_buf, x_sem)
    x_copy.start()
    for t in range(tiles - 1):
        pltpu.make_async_copy(wq_any.at[:, pl.ds(t * tile, tile)], w_buf.at[t], w_sem.at[t]).start()
    k_copy = pltpu.make_async_copy(wk_any, w_buf.at[tiles - 1, :, pl.ds(0, head_dim)], w_sem.at[tiles - 1])
    v_copy = pltpu.make_async_copy(wv_any, w_buf.at[tiles - 1, :, pl.ds(head_dim, head_dim)], w_sem.at[tiles])
    k_copy.start()
    v_copy.start()
    x_copy.wait()
    gain = vec_ref[0:1, :]
    shift = vec_ref[1:2, :]

    def norm_rows(i, carry):
        at = pl.ds(pl.multiple_of(i * 16, 16), 16)
        vals = x_buf[at, :].astype(F32)
        mean = jnp.sum(vals, axis=-1, keepdims=True) * (1.0 / width)
        vals = vals - mean
        var = jnp.sum(vals * vals, axis=-1, keepdims=True) * (1.0 / width)
        hid[at, :] = (vals * lax.rsqrt(var + LN_EPS) * gain + shift).astype(BF16)
        return carry

    lax.fori_loop(0, rows // 16, norm_rows, 0)
    perm = one_hot_rows(rows, batch)
    cos_t = cos_ref[...]
    sin_t = sin_ref[...]

    def one_tile(t, carry):
        acc = jnp.dot(hid[...], w_buf[t], preferred_element_type=F32) + bias_ref[t]
        acc = acc.astype(BF16).astype(F32)
        for part in range(2):
            vals = acc[:, part * head_dim:(part + 1) * head_dim]
            cos_p, sin_p = cos_t, sin_t
            if part == 1:
                cos_p = jnp.where(t == tiles - 1, 1.0, cos_t)
                sin_p = jnp.where(t == tiles - 1, 0.0, sin_t)
            vals = vals * cos_p + pltpu.roll(vals, head_dim // 2, 1) * sin_p
            out_ref[2 * t + part] = jnp.dot(perm, vals.astype(BF16), preferred_element_type=F32)
        return carry

    def q_tile(t, carry):
        pltpu.make_async_copy(wq_any.at[:, pl.ds(pl.multiple_of(t * tile, tile), tile)], w_buf.at[t], w_sem.at[t]).wait()
        return one_tile(t, carry)

    lax.fori_loop(0, tiles - 1, q_tile, 0)
    k_copy.wait()
    v_copy.wait()
    lax.fori_loop(tiles - 1, tiles, one_tile, 0)


def attend_kernel(pos_ref, where_ref, qkv_ref, k_ref, v_ref, part_ref, kout_ref, vout_ref, *,
                  heads, steps, slots):
    batches, local, head_dim = k_ref.shape
    half = heads // 2
    first = where_ref[0]
    leader = where_ref[1]
    base_batch = pl.program_id(0) * batches
    kout_ref[...] = k_ref[...]
    vout_ref[...] = v_ref[...]
    scale = head_dim ** -0.5
    pair_rows = 2 * steps
    row = lax.broadcasted_iota(jnp.int32, (pair_rows, local), 0)
    slot = lax.broadcasted_iota(jnp.int32, (pair_rows, local), 1) + first
    step = lax.rem(row, steps)
    n_row = lax.broadcasted_iota(jnp.int32, (pair_rows, head_dim), 0)
    n_col = lax.broadcasted_iota(jnp.int32, (pair_rows, head_dim), 1)
    new_ok = ((lax.div(n_row, steps) == lax.div(n_col, steps)) & (lax.rem(n_col, steps) <= lax.rem(n_row, steps))
              & (n_col < pair_rows) & (leader == 1))
    lane = n_col
    pad = jnp.zeros((head_dim - pair_rows, head_dim), F32)
    nt = (((1,), (1,)), ((), ()))
    for pr in range(batches // 2):
        rows = slice(pair_rows * pr, pair_rows * (pr + 1))
        pos0 = pos_ref[base_batch + 2 * pr]
        pos1 = pos_ref[base_batch + 2 * pr + 1]
        cur = jnp.where(row < steps, pos0, pos1) + step
        dist = lax.rem(cur - slot + slots * (1 + (1 << 20) // slots), slots) if slots & (slots - 1) else (cur - slot) & (slots - 1)
        old_ok = ((dist > step) & (dist <= cur))[None]
        query = qkv_ref[0:heads, rows, :].reshape(heads * pair_rows, head_dim).astype(BF16)
        new_k = jnp.concatenate([qkv_ref[heads, rows, :], pad], axis=0).astype(BF16)
        new_v = jnp.concatenate([qkv_ref[heads + 1, rows, :], pad], axis=0).astype(BF16)
        score0 = lax.dot_general(query, k_ref[2 * pr], nt, preferred_element_type=F32).reshape(heads, pair_rows, local)
        score1 = lax.dot_general(query, k_ref[2 * pr + 1], nt, preferred_element_type=F32).reshape(heads, pair_rows, local)
        score = jnp.where((row < steps)[None], score0, score1) * scale
        score = jnp.where(old_ok, score, NEG_BIG)
        score_n = lax.dot_general(query, new_k, nt, preferred_element_type=F32).reshape(heads, pair_rows, head_dim) * scale
        score_n = jnp.where(new_ok[None], score_n, NEG_BIG)
        top = jnp.maximum(jnp.max(score, axis=-1, keepdims=True), jnp.max(score_n, axis=-1, keepdims=True))
        wts = jnp.where(old_ok, jnp.exp(score - top), 0.0)
        wts_n = jnp.where(new_ok[None], jnp.exp(score_n - top), 0.0)
        total = jnp.sum(wts, axis=-1, keepdims=True) + jnp.sum(wts_n, axis=-1, keepdims=True)
        wts = wts.reshape(heads * pair_rows, local).astype(BF16)
        wts_n = wts_n.reshape(heads * pair_rows, head_dim).astype(BF16)
        out0 = jnp.dot(wts, v_ref[2 * pr], preferred_element_type=F32).reshape(heads, pair_rows, head_dim)
        out1 = jnp.dot(wts, v_ref[2 * pr + 1], preferred_element_type=F32).reshape(heads, pair_rows, head_dim)
        out_n = jnp.dot(wts_n, new_v, preferred_element_type=F32).reshape(heads, pair_rows, head_dim)
        out = jnp.where((n_row < steps)[None], out0, out1) + out_n
        for core in range(2):
            part_ref[core, 0:half, rows, :] = out[core * half:(core + 1) * half]
            stat = jnp.zeros((pair_rows, head_dim), F32)
            for h in range(half):
                stat = jnp.where(lane == h, top[core * half + h], stat)
                stat = jnp.where(lane == head_dim // 2 + h, total[core * half + h], stat)
            part_ref[core, half, rows, :] = stat
    window = lax.broadcasted_iota(jnp.int32, (16, head_dim), 0)
    for b in range(batches):
        for t in range(steps):
            full = lax.rem(pos_ref[base_batch + b] + t, slots)
            at = full - first

            @pl.when((at >= 0) & (at < local))
            def _():
                start = pl.multiple_of(lax.div(at, 16) * 16, 16)
                hit = window == at - start
                for src, dst in ((heads, kout_ref), (heads + 1, vout_ref)):
                    fresh = qkv_ref[src, b * steps + t:b * steps + t + 1, :]
                    old = dst[b, pl.ds(start, 16), :].astype(F32)
                    dst[b, pl.ds(start, 16), :] = jnp.where(hit, fresh, old).astype(BF16)


def merge_parts(parts, half, head_dim):
    stats = [p[half] for p in parts]
    top = functools.reduce(jnp.maximum, stats)
    scales = [jnp.exp(s - top) for s in stats]
    lane = lax.broadcasted_iota(jnp.int32, top.shape, 1)
    total = sum(s * pltpu.roll(f, head_dim // 2, 1) for s, f in zip(stats, scales))
    stat = jnp.where(lane < head_dim // 2, top, total)
    outs = []
    for h in range(half):
        outs.append(sum(p[h] * f[:, h:h + 1] for p, f in zip(parts, scales)))
    return outs, stat


def tail_kernel(part_ref, x_any, vec_ref, bfc_ref, wo_any, wfc_any, wpj_any, y_ref,
                w_buf, x_buf, merged, pair_in, x_in, a_own, a_in, a_full, o_part, o_in, x1_all, hid, f_acc,
                g_own, g_in, p_part, p_in, y_all, w_sem, x_sem, send, recv, *, n_x, n_y, half, head_dim, col_tile):
    steps, blk_b, cols = x_buf.shape
    blk = steps * blk_b
    width = n_y * 2 * cols
    core_cols = n_y * cols
    depth = w_buf.shape[1]
    sq = lax.axis_index("sq")
    y = lax.axis_index("tp")
    x = lax.div(sq, 2)
    c = lax.rem(sq, 2)
    mine = c * n_y + y
    my_col = pl.multiple_of(mine * cols, cols)
    half_col = pl.multiple_of(c * core_cols, core_cols)

    def partner():
        return {"tp": y, "sq": 2 * x + 1 - c}

    def along_x(d):
        return {"tp": y, "sq": 2 * lax.rem(x + d, n_x) + c}

    def along_y(d):
        return {"tp": lax.rem(y + d, n_y), "sq": sq}

    ids = iter(range(1000))

    def remote(src, dst, dev):
        n = next(ids)
        return pltpu.make_async_remote_copy(src_ref=src, dst_ref=dst, send_sem=send.at[n], recv_sem=recv.at[n],
                                            device_id=dev, device_id_type=MESH)

    fc_rows = width // 4
    pj_rows = wpj_any.shape[0] // 4
    wo_copy = pltpu.make_async_copy(wo_any.at[:, pl.ds(half_col, core_cols)], w_buf.at[0], w_sem.at[0])
    fc_copy = [pltpu.make_async_copy(wfc_any.at[pl.ds(k * fc_rows, fc_rows), pl.ds(half_col, core_cols)], w_buf.at[1 + k],
                                     w_sem.at[1 + k]) for k in range(4)]
    pj_copy = []
    for k in range(4):
        side = c if k < 2 else 1 - c
        start = pl.multiple_of(side * (2 * pj_rows) + (k % 2) * pj_rows, 16)
        pj_copy.append(pltpu.make_async_copy(wpj_any.at[pl.ds(start, pj_rows), pl.ds(half_col, core_cols)], w_buf.at[k],
                                             w_sem.at[5 + k]))
    x_copy = pltpu.make_async_copy(x_any.at[:, pl.ds(pl.multiple_of(x * blk_b, blk_b), blk_b), pl.ds(my_col, cols)], x_buf, x_sem)
    x_copy.start()
    wo_copy.start()
    fc_copy[0].start()

    barrier = pltpu.get_barrier_semaphore()
    peers = [partner()] + [along_x(d) for d in range(1, n_x)] + [along_y(d) for d in range(1, n_y)]
    for dev in peers:
        pl.semaphore_signal(barrier, inc=1, device_id=dev, device_id_type=MESH)
    pl.semaphore_wait(barrier, len(peers))

    sent = []
    pair = remote(part_ref.at[1 - c], pair_in, partner())
    pair.start()
    sent.append(pair)
    pair.wait_recv()
    hops = []
    for d in list(range(1, n_x)) + [0]:
        at = pl.ds(pl.multiple_of(lax.rem(x + d, n_x) * blk, blk), blk)
        own = [part_ref[c, h, at, :] for h in range(half + 1)]
        other = [pair_in[h, at, :] for h in range(half + 1)]
        outs, stat = merge_parts([own, other], half, head_dim)
        for h in range(half):
            merged[h, at, :] = outs[h]
        merged[half, at, :] = stat
        if d:
            hop = remote(merged.at[:, at, :], x_in.at[d - 1], along_x(d))
            hop.start()
            hops.append(hop)
    fc_copy[1].start()
    fc_copy[2].start()
    for hop in hops:
        hop.wait_recv()
    sent += hops
    at = pl.ds(pl.multiple_of(x * blk, blk), blk)
    parts = [[merged[h, at, :] for h in range(half + 1)]]
    for d in range(n_x - 1):
        parts.append([x_in[d, h] for h in range(half + 1)])
    outs, stat = merge_parts(parts, half, head_dim)
    for h in range(half):
        denom = stat[:, head_dim // 2 + h:head_dim // 2 + h + 1]
        a_own[:, h * head_dim:(h + 1) * head_dim] = (outs[h] / denom).astype(BF16).astype(F32)
    a_copy = remote(a_own, a_in, partner())
    a_copy.start()
    sent.append(a_copy)
    fc_copy[3].start()
    perm = one_hot_rows(blk, steps)
    a_cols = half * head_dim
    a_full[:, pl.ds(pl.multiple_of(c * a_cols, a_cols), a_cols)] = jnp.dot(
        perm, a_own[...].astype(BF16), preferred_element_type=F32).astype(BF16)
    a_copy.wait_recv()
    a_full[:, pl.ds(pl.multiple_of((1 - c) * a_cols, a_cols), a_cols)] = jnp.dot(
        perm, a_in[...].astype(BF16), preferred_element_type=F32).astype(BF16)

    wo_copy.wait()
    order = [d for d in (2, 1, 3) if d < n_y] + [d for d in range(4, n_y)] + [0]
    hops = {}
    for d in order:
        at = pl.ds(pl.multiple_of(lax.rem(y + d, n_y) * cols, cols), cols)
        o_part[:, at] = jnp.dot(a_full[...], w_buf[0, :, at], preferred_element_type=F32)
        if d:
            hops[d] = remote(o_part.at[:, at], o_in.at[d - 1], along_y(d))
            hops[d].start()
    pj_copy[0].start()
    x_copy.wait()
    at = pl.ds(pl.multiple_of(y * cols, cols), cols)
    acc = o_part[:, at]
    for d in order[:-1]:
        hops[d].wait_recv()
        sent.append(hops[d])
        acc = acc + o_in[d - 1]
    x_mid = x_buf[...].astype(F32).reshape(blk, cols) + acc + vec_ref[2:3, pl.ds(my_col, cols)]
    x1_all[mine] = x_mid.astype(BF16).astype(F32)

    hops = [remote(x1_all.at[mine], x1_all.at[mine], along_y(d)) for d in range(1, n_y)]
    for hop in hops:
        hop.start()
    fwd = [remote(x1_all.at[mine], x1_all.at[mine], partner())]
    fwd[0].start()
    for d in range(1, n_y):
        hops[d - 1].wait_recv()
        slot = c * n_y + lax.rem(y - d + n_y, n_y)
        fwd.append(remote(x1_all.at[slot], x1_all.at[slot], partner()))
        fwd[-1].start()
    for hop in fwd:
        hop.wait_recv()
    sent += hops + fwd

    total = jnp.zeros((blk, 1), F32)
    for i in range(2 * n_y):
        total = total + jnp.sum(x1_all[i], axis=-1, keepdims=True)
    mean = total * (1.0 / width)
    total = jnp.zeros((blk, 1), F32)
    for i in range(2 * n_y):
        dev = x1_all[i] - mean
        total = total + jnp.sum(dev * dev, axis=-1, keepdims=True)
    inv = lax.rsqrt(total * (1.0 / width) + LN_EPS)
    for i in range(2 * n_y):
        at = slice(i * cols, (i + 1) * cols)
        hid[:, at] = ((x1_all[i] - mean) * inv * vec_ref[4:5, at] + vec_ref[5:6, at]).astype(BF16)

    tiles = core_cols // col_tile
    for k in range(4):
        fc_copy[k].wait()

        def fc_tile(j, carry, k=k):
            at = pl.ds(pl.multiple_of(j * col_tile, col_tile), col_tile)
            val = jnp.dot(hid[:, k * fc_rows:(k + 1) * fc_rows], w_buf[1 + k, :, at], preferred_element_type=F32)
            if k > 0:
                val = val + f_acc[:, at]
            if k < 3:
                f_acc[:, at] = val
            else:
                val = val + bfc_ref[:, pl.ds(pl.multiple_of(half_col + j * col_tile, col_tile), col_tile)]
                g_own[:, at] = jax.nn.gelu(val, approximate=True).astype(BF16).astype(F32)
            return carry

        lax.fori_loop(0, tiles, fc_tile, 0)
        if k < 3:
            pj_copy[k + 1].start()
    g_copy = remote(g_own, g_in, partner())
    g_copy.start()
    sent.append(g_copy)
    for k in range(3):
        if k == 2:
            g_copy.wait_recv()
        pj_copy[k].wait()
        left = g_own if k < 2 else g_in

        def pj_tile(j, carry, k=k, left=left):
            at = pl.ds(pl.multiple_of(j * col_tile, col_tile), col_tile)
            lhs = left[:, (k % 2) * pj_rows:(k % 2 + 1) * pj_rows].astype(BF16)
            val = jnp.dot(lhs, w_buf[k, :, at], preferred_element_type=F32)
            if k > 0:
                val = val + p_part[:, at]
            p_part[:, at] = val
            return carry

        lax.fori_loop(0, tiles, pj_tile, 0)
    pj_copy[3].wait()
    hops = {}
    for d in order:
        at = pl.ds(pl.multiple_of(lax.rem(y + d, n_y) * cols, cols), cols)
        p_part[:, at] = p_part[:, at] + jnp.dot(g_in[:, pj_rows:2 * pj_rows].astype(BF16), w_buf[3, :, at],
                                                preferred_element_type=F32)
        if d:
            hops[d] = remote(p_part.at[:, at], p_in.at[d - 1], along_y(d))
            hops[d].start()
    at = pl.ds(pl.multiple_of(y * cols, cols), cols)
    acc = p_part[:, at]
    for d in order[:-1]:
        hops[d].wait_recv()
        sent.append(hops[d])
        acc = acc + p_in[d - 1]
    y_all[x, mine] = (x1_all[mine] + acc + vec_ref[3:4, pl.ds(my_col, cols)]).astype(BF16).astype(F32)

    upper, lower = pl.ds(0, blk // 2), pl.ds(blk // 2, blk // 2)
    own_slots = pl.ds(c * n_y, n_y)
    up1, low1 = [], []
    for d in range(1, max(n_x, n_y)):
        if d < n_x:
            up1.append(remote(y_all.at[x, mine, upper], y_all.at[x, mine, upper], along_x(d)))
            up1[-1].start()
        if d < n_y:
            low1.append(remote(y_all.at[x, mine, lower], y_all.at[x, mine, lower], along_y(d)))
            low1[-1].start()
    for hop in up1:
        hop.wait_recv()
    view = y_all.at[:, mine, upper]
    up2 = [remote(view, view, along_y(d)) for d in range(1, n_y)]
    for hop in up2:
        hop.start()
    fwd = [remote(view, view, partner())]
    for hop in low1:
        hop.wait_recv()
    view = y_all.at[x, own_slots, lower]
    low2 = [remote(view, view, along_x(d)) for d in range(1, n_x)]
    for hop in low2:
        hop.start()
    fwd.append(remote(view, view, partner()))
    fwd[0].start()
    fwd[1].start()
    for d in range(1, max(n_x, n_y)):
        if d < n_y:
            up2[d - 1].wait_recv()
            view = y_all.at[:, c * n_y + lax.rem(y - d + n_y, n_y), upper]
            fwd.append(remote(view, view, partner()))
            fwd[-1].start()
        if d < n_x:
            low2[d - 1].wait_recv()
            view = y_all.at[lax.rem(x - d + n_x, n_x), own_slots, lower]
            fwd.append(remote(view, view, partner()))
            fwd[-1].start()
    for hop in fwd:
        hop.wait_recv()
    sent += up1 + low1 + up2 + low2 + fwd
    for s in range(steps):
        for xb in range(0, n_x, 2):
            for i in range(2 * n_y):
                block = jnp.concatenate([y_all[xb, i, s * blk_b:(s + 1) * blk_b, :],
                                         y_all[xb + 1, i, s * blk_b:(s + 1) * blk_b, :]], axis=0)
                y_ref[s, xb * blk_b:(xb + 2) * blk_b, i * cols:(i + 1) * cols] = block.astype(BF16)
    for hop in sent:
        hop.wait_send()


def solution(mesh):
    n_sq = mesh.shape["sq"]
    n_y = mesh.shape["tp"]
    n_x = n_sq // 2
    act_spec = P(None, "dp", None)
    cache_spec = P("dp", "sq", "tp", None)
    col_spec = P(None, "tp")
    row_spec = P("tp", None)
    vec_spec = P("tp")
    rep_spec = P(None)
    in_specs = (act_spec, P("dp"), cache_spec, cache_spec, col_spec, vec_spec, col_spec, vec_spec,
                col_spec, vec_spec, row_spec, rep_spec, rep_spec, rep_spec, rep_spec, rep_spec,
                col_spec, vec_spec, row_spec, rep_spec)
    out_specs = (act_spec, cache_spec, cache_spec)
    vmem = pl.BlockSpec(memory_space=pltpu.VMEM)
    hbm = pl.BlockSpec(memory_space=pl.ANY)

    def per_device(x_steps, positions, key_buf, val_buf, w_q, b_q, w_k, b_k, w_v, b_v, w_o, b_o,
                   ln1_gain, ln1_bias, ln2_gain, ln2_bias, w_fc, b_fc, w_proj, b_proj):
        steps, batch, width = x_steps.shape
        local, head_dim = key_buf.shape[1], key_buf.shape[3]
        slots = local * n_sq
        rows = steps * batch
        heads = w_q.shape[1] // head_dim
        half = heads // 2
        tile = 2 * head_dim
        tiles = w_q.shape[1] // tile + 1
        vecs = jnp.stack([ln1_gain, ln1_bias, b_o, b_proj, ln2_gain, ln2_bias]).astype(F32)
        qkv_bias = jnp.concatenate([b_q, b_k, b_v]).astype(F32).reshape(tiles, 1, tile)
        half_dim = head_dim // 2
        inv_freq = jnp.power(jnp.float32(ROPE_BASE), -2.0 * jnp.arange(half_dim, dtype=F32) / head_dim)
        cur = positions[None, :] + jnp.arange(steps, dtype=jnp.int32)[:, None]
        angle = cur.reshape(rows).astype(F32)[:, None] * inv_freq
        cos_t, sin_t = jnp.cos(angle), jnp.sin(angle)
        cos_t = jnp.concatenate([cos_t, cos_t], axis=-1)
        sin_t = jnp.concatenate([-sin_t, sin_t], axis=-1)

        qkv = pl.pallas_call(
            functools.partial(qkv_kernel, batch=batch, tiles=tiles, tile=tile, head_dim=head_dim),
            out_shape=jax.ShapeDtypeStruct((heads + 2, rows, head_dim), F32),
            in_specs=[hbm, hbm, hbm, hbm, vmem, vmem, vmem, vmem],
            out_specs=vmem,
            scratch_shapes=[pltpu.VMEM((rows, width), BF16), pltpu.VMEM((tiles, width, tile), BF16),
                            pltpu.VMEM((rows, width), BF16), pltpu.SemaphoreType.DMA,
                            pltpu.SemaphoreType.DMA((tiles + 1,))],
            compiler_params=pltpu.CompilerParams(vmem_limit_bytes=VMEM_BYTES),
            name="qkv",
        )(x_steps.reshape(rows, width), w_q, w_k, w_v, qkv_bias, vecs, cos_t, sin_t)

        sq = lax.axis_index("sq")
        place = jnp.stack([sq * local, jnp.where(sq == 0, 1, 0)]).astype(jnp.int32)
        per = 4
        kv_spec = pl.BlockSpec((per, local, head_dim), lambda i, *_: (i, 0, 0))
        part, k_new, v_new = pl.pallas_call(
            functools.partial(attend_kernel, heads=heads, steps=steps, slots=slots),
            out_shape=(jax.ShapeDtypeStruct((2, half + 1, rows, head_dim), F32),
                       jax.ShapeDtypeStruct((batch, local, head_dim), BF16),
                       jax.ShapeDtypeStruct((batch, local, head_dim), BF16)),
            grid_spec=pltpu.PrefetchScalarGridSpec(
                num_scalar_prefetch=2, grid=(batch // per,),
                in_specs=[pl.BlockSpec((heads + 2, per * steps, head_dim), lambda i, *_: (0, i, 0)), kv_spec, kv_spec],
                out_specs=(pl.BlockSpec((2, half + 1, per * steps, head_dim), lambda i, *_: (0, 0, i, 0)), kv_spec, kv_spec)),
            compiler_params=pltpu.CompilerParams(dimension_semantics=("arbitrary",), vmem_limit_bytes=VMEM_BYTES),
            name="attend",
        )(positions, place, qkv, key_buf.reshape(batch, local, head_dim), val_buf.reshape(batch, local, head_dim))

        cols = width // (2 * n_y)
        core_cols = width // 2
        blk_b = batch // n_x
        blk = blk_b * steps
        depth = w_o.shape[0]
        ys = pl.pallas_call(
            functools.partial(tail_kernel, n_x=n_x, n_y=n_y, half=half, head_dim=head_dim, col_tile=min(512, core_cols)),
            out_shape=jax.ShapeDtypeStruct((steps, batch, width), BF16),
            in_specs=[vmem, hbm, vmem, vmem, hbm, hbm, hbm],
            out_specs=vmem,
            scratch_shapes=[
                pltpu.VMEM((5, depth, core_cols), BF16),
                pltpu.VMEM((steps, blk_b, cols), BF16),
                pltpu.VMEM((half + 1, rows, head_dim), F32),
                pltpu.VMEM((half + 1, rows, head_dim), F32),
                pltpu.VMEM((n_x - 1, half + 1, blk, head_dim), F32),
                pltpu.VMEM((blk, half * head_dim), F32),
                pltpu.VMEM((blk, half * head_dim), F32),
                pltpu.VMEM((blk, heads * head_dim), BF16),
                pltpu.VMEM((blk, core_cols), F32),
                pltpu.VMEM((n_y - 1, blk, cols), F32),
                pltpu.VMEM((2 * n_y, blk, cols), F32),
                pltpu.VMEM((blk, width), BF16),
                pltpu.VMEM((blk, core_cols), F32),
                pltpu.VMEM((blk, core_cols), F32),
                pltpu.VMEM((blk, core_cols), F32),
                pltpu.VMEM((blk, core_cols), F32),
                pltpu.VMEM((n_y - 1, blk, cols), F32),
                pltpu.VMEM((n_x, 2 * n_y, blk, cols), F32),
                pltpu.SemaphoreType.DMA((9,)),
                pltpu.SemaphoreType.DMA,
                pltpu.SemaphoreType.DMA((48,)),
                pltpu.SemaphoreType.DMA((48,)),
            ],
            compiler_params=pltpu.CompilerParams(collective_id=0, has_side_effects=True, vmem_limit_bytes=VMEM_BYTES),
            name="tail",
        )(part, x_steps, vecs, b_fc.astype(F32).reshape(1, -1), w_o, w_fc, w_proj)
        return ys, k_new.reshape(key_buf.shape), v_new.reshape(val_buf.shape)

    return jax.shard_map(per_device, mesh=mesh, in_specs=in_specs, out_specs=out_specs, check_vma=False)
```

time: 597 us -> 125 us (0.21); the launches traced: 589 us -> 124 us
  matrix products: 320 us -> 0 us
  waiting for transfers between devices: 149 us -> 0 us
  Pallas kernels: 0 us -> 111 us
  local copies, waits for them, and re-layouts: 68.3 us -> 7.94 us
  other arithmetic: 34 us -> 5.11 us
  between operations: 15.7 us -> 0.69 us
    dot_general x32 -> x0, matrix products: 320 us -> none  [the longest x16 159 us: linear(): jnp.dot(rows_in, weight, preferred_element_type=jnp.float32)]
    psum x2 -> x0, waiting for transfers between devices: 139 us -> none  [the longest x1 69.5 us: layer_tail(): lax.psum(jnp.dot(attn_out, w_o, preferred_element_type=jnp.float32), 'tp')]
    pallas_call x0 -> x3, Pallas kernels: none -> 111 us  [the longest x1 78.6 us: per_device(): pl.pallas_call(functools.partial(tail_kernel, n_x=n_x, n_y=n_y, half=half...]
    scatter x8 -> x0, local copies, waits for them, and re-layouts: 35.4 us -> none  [the longest x4 17.7 us: per_device(): val_buf = val_buf.at[batch_ids, local_slot].set(v_heads, mode='drop')]
    all_gather x4 -> x0, local copies, waits for them, and re-layouts: 13.6 us -> none  [per_device(): gathered = lax.all_gather(stats, 'sq')]
    reduce_sum x19 -> x0, other arithmetic: 10.6 us -> none  [the longest x2 4 us: layer_norm(): row_mean = jnp.mean(vectors, axis=-1, keepdims=True)]
    all_gather x4 -> x0, waiting for transfers between devices: 10.2 us -> none  [per_device(): gathered = lax.all_gather(stats, 'sq')]
    slice x4 -> x0, other arithmetic: 7.62 us -> none  [per_device(): all_max = gathered[..., head_dim + 1]]
  transfers between devices with their start and end apart: 6 -> 0, of which waited for: 3 -> 0; matrix products, arithmetic and copies ran while one was open for 19% -> 0% of each run, Pallas kernels for 0% -> 0%
where the time goes in v1:
time: 125 us; the launch traced here: 124 us
  Pallas kernels  111 us (89%)
  local copies, waits for them, and re-layouts  7.94 us (6%)
  other arithmetic  5.11 us (4%)
    pallas_call x1, Pallas kernels, per_device(): pl.pallas_call(functools.partial(tail_kernel, n_x=n_x, n_y=n_y, half=half...  78.6 us
    pallas_call x1, Pallas kernels, per_device(): pl.pallas_call(functools.partial(qkv_kernel, batch=batch, tiles=tiles, ti...  18 us
    pallas_call x1, Pallas kernels, per_device(): pl.pallas_call(functools.partial(attend_kernel, heads=heads, steps=steps,...  14 us
    another operation x7, local copies, waits for them, and re-layouts, per_device(): jnp.stack([ln1_gain, ln1_bias, b_o, b_proj, ln2_gain, ln2_bias]).astype(F32)  4.56 us
    unnamed x1, local copies, waits for them, and re-layouts  2.69 us

profile of v1, /device:TPU:97, one launch (start us, length us, event | category | flops | bytes accessed | tf_op | source)
XLA Modules:
  0.0 124.3 jit_solution(11301310825160031349)
XLA Ops:
  0.6 0.6 pad_add_fusion.where_ref
  1.3 0.7 add_convert_fusion
  1.9 0.1 convert_element_type.31
  2.0 0.7 maximum_convert_fusion
  2.7 0.6 reshape.67.bias_ref
  3.4 0.7 stack.35
  4.1 0.7 stack.33
  4.8 0.7 stack.34
  5.5 0.7 stack.37
  6.3 0.7 stack.38
  7.0 1.3 %reshape.68 = f32[6144]{0:T(1024)} convert(bf16[6144]{0:T(1024)(128)(2,1)} %param.37) | non-fusion elementwise | flops 6144 | bytes 36864 | tf_op jit(solution)/shard_map/reshape | solution.py:513
  8.3 0.7 stack.36
  9.0 0.2 stack.39
  9.3 0.7 convert_element_type.29.vec_ref
  10.0 0.3 fusion
  10.3 0.8 pad_maximum_fusion
  11.0 18.0 %qkv.1.qkv_ref = f32[14,128,128]{2,1,0:T(8,128)} custom-call(bf16[128,6144]{1,0:T(8,128)(2,1)} %bitcast.12, bf16[6144,1536]{1,0:T(8,128)(2,1)} %wq_any.1, bf16[6144,128]{1,0:T(8,128)(2,1)} %wk_any.1, bf16[6144,128]{1,0:T(8,128)(2,1)} %wv_any.1, f32[7,1,256]{2,1,0:T(1,128)} %reshape.67.bias_ref, f32[6,6144]{1,0:T(8,128)} %convert_element_type.29.vec_ref, ...), custom_call_target="tpu_custom_call" | custom-call | tf_op jit(solution)/shard_map/qkv/pallas_call | solution.py:448
  29.1 14.0 %attend.1 = (f32[2,7,128,128]{3,2,1,0:T(8,128)}, bf16[32,512,128]{2,1,0:T(8,128)(2,1)}, bf16[32,512,128]{2,1,0:T(8,128)(2,1)}) custom-call(s32[32]{0:T(128)} %pos_ref.1, s32[2]{0:T(128)} %pad_add_fusion.where_ref, f32[14,128,128]{2,1,0:T(8,128)} %qkv.1.qkv_ref, bf16[32,512,128]{2,1,0:T(8,128)(2,1)} %bitcast.13, bf16[32,512,128]{2,1,0:T(8,128)(2,1)} %bitcast.14), custom_call_target="tpu_custom_call" | custom-call | tf_op jit(solution)/shard_map/attend/pallas_call | solution.py:464
  43.0 78.6 %tail.1 = bf16[4,32,6144]{2,1,0:T(8,128)(2,1)} custom-call(f32[2,7,128,128]{3,2,1,0:T(8,128)} %get-tuple-element.6.part_ref, bf16[4,32,6144]{2,1,0:T(8,128)(2,1)} %x_any.1, f32[6,6144]{1,0:T(8,128)} %convert_element_type.29.vec_ref, f32[1,6144]{1,0:T(1,128)} %bitcast.15, bf16[1536,6144]{1,0:T(8,128)(2,1)} %wo_any.1, bf16[6144,6144]{1,0:T(8,128)(2,1)} %wfc_any.1, ...), custom_call_target="tpu_custom_call" | custom-call | tf_op jit(solution)/shard_map/tail/pallas_call | solution.py:482
  121.7 2.7 %copy.26 = bf16[4,32,6144]{2,1,0:T(8,128)(2,1)} copy(bf16[4,32,6144]{2,1,0:T(8,128)(2,1)} %tail.1) | data formatting | bytes 3145728
  (1 shorter events, 0.0 us)

commit v2 on v0

v2 whole, which is shorter than its diff:
```python
import functools

import jax
import jax.numpy as jnp
from jax import lax
from jax.experimental import pallas as pl
from jax.experimental.pallas import tpu as pltpu
from jax.sharding import PartitionSpec as P

ROPE_BASE = 1000000.0
LN_EPS = 1e-5
NEG_BIG = -1e30
MESH = pl.DeviceIdType.MESH
F32 = jnp.float32
BF16 = jnp.bfloat16
VMEM_BYTES = 67043328


def one_hot_rows(size, inner):
    outer = size // inner
    row = lax.broadcasted_iota(jnp.int32, (size, size), 0)
    col = lax.broadcasted_iota(jnp.int32, (size, size), 1)
    source = lax.rem(row, outer) * inner + lax.div(row, outer)
    return jnp.where(col == source, 1.0, 0.0).astype(BF16)


def front_kernel(pos_ref, x_any, wq_any, wk_any, wv_any, vec_ref, cos_ref, sin_ref, kc_any, vc_any,
                 part_ref, kout_any, vout_any,
                 x_buf, hid, wq_buf, wk_buf, wv_buf, acc, qkv, k_buf, v_buf,
                 x_sem, wq_sem, kv_sem, c_sem, out_sem, *, batch, heads, head_dim, steps, per):
    rows, width = x_buf.shape
    n_q = heads * head_dim
    bands, band = wq_buf.shape[0], wq_buf.shape[1]
    local = k_buf.shape[1]
    slots = local * lax.axis_size("sq")
    groups = batch // per
    half = heads // 2
    first = lax.axis_index("sq") * local
    leader = lax.axis_index("sq") == 0

    x_copy = pltpu.make_async_copy(x_any, x_buf, x_sem)
    x_copy.start()
    k_copy = pltpu.make_async_copy(wk_any, wk_buf, kv_sem.at[0])
    v_copy = pltpu.make_async_copy(wv_any, wv_buf, kv_sem.at[1])
    k_copy.start()
    v_copy.start()

    def q_copy(i):
        return pltpu.make_async_copy(wq_any.at[pl.ds(pl.multiple_of(i * band, band), band), :], wq_buf.at[i], wq_sem.at[i])

    def cache_in(i):
        at = pl.ds(i * per, per)
        return (pltpu.make_async_copy(kc_any.at[at], k_buf.at[at], c_sem.at[0, i]),
                pltpu.make_async_copy(vc_any.at[at], v_buf.at[at], c_sem.at[1, i]))

    def cache_out(i):
        at = pl.ds(i * per, per)
        return (pltpu.make_async_copy(k_buf.at[at], kout_any.at[at], out_sem.at[0, i]),
                pltpu.make_async_copy(v_buf.at[at], vout_any.at[at], out_sem.at[1, i]))

    for i in range(bands):
        q_copy(i).start()
    for i in range(groups):
        for cp in cache_in(i):
            cp.start()

    gain = vec_ref[0:1, 0:width]
    shift = vec_ref[0:1, width:2 * width]
    x_copy.wait()

    def norm_rows(i, carry):
        at = pl.ds(pl.multiple_of(i * 16, 16), 16)
        vals = x_buf[at, :].astype(F32)
        mean = jnp.sum(vals, axis=-1, keepdims=True) * (1.0 / width)
        vals = vals - mean
        var = jnp.sum(vals * vals, axis=-1, keepdims=True) * (1.0 / width)
        hid[at, :] = (vals * lax.rsqrt(var + LN_EPS) * gain + shift).astype(BF16)
        return carry

    lax.fori_loop(0, rows // 16, norm_rows, 0)

    bias0 = vec_ref.shape[1] - n_q - 2 * head_dim
    perm = one_hot_rows(rows, batch)
    cos_t = cos_ref[...]
    sin_t = sin_ref[...]

    def rotate(vals):
        return vals * cos_t + pltpu.roll(vals, head_dim // 2, 1) * sin_t

    def by_batch(vals):
        return jnp.dot(perm, vals.astype(BF16), preferred_element_type=F32)

    k_copy.wait()
    v_copy.wait()
    k_new = jnp.dot(hid[...], wk_buf[...], preferred_element_type=F32) + vec_ref[0:1, bias0 + n_q:bias0 + n_q + head_dim]
    v_new = jnp.dot(hid[...], wv_buf[...], preferred_element_type=F32) + vec_ref[0:1, bias0 + n_q + head_dim:]
    qkv[heads] = by_batch(rotate(k_new.astype(BF16).astype(F32)))
    qkv[heads + 1] = by_batch(v_new)
    acc[...] = jnp.broadcast_to(vec_ref[0:1, bias0:bias0 + n_q], acc.shape)

    def q_band(i, carry):
        q_copy(i).wait()
        acc[...] += jnp.dot(hid[:, pl.ds(pl.multiple_of(i * band, band), band)], wq_buf[i], preferred_element_type=F32)
        return carry

    lax.fori_loop(0, bands, q_band, 0)

    def q_head(h, carry):
        vals = acc[:, pl.ds(pl.multiple_of(h * head_dim, head_dim), head_dim)]
        qkv[h] = by_batch(rotate(vals.astype(BF16).astype(F32)))
        return carry

    lax.fori_loop(0, heads, q_head, 0)

    scale = head_dim ** -0.5
    pair_rows = 2 * steps
    row = lax.broadcasted_iota(jnp.int32, (pair_rows, local), 0)
    slot = lax.broadcasted_iota(jnp.int32, (pair_rows, local), 1) + first
    step = lax.rem(row, steps)
    n_row = lax.broadcasted_iota(jnp.int32, (pair_rows, head_dim), 0)
    n_col = lax.broadcasted_iota(jnp.int32, (pair_rows, head_dim), 1)
    new_ok = ((lax.div(n_row, steps) == lax.div(n_col, steps)) & (lax.rem(n_col, steps) <= lax.rem(n_row, steps))
              & (n_col < pair_rows) & leader)[None]
    lane = n_col
    pad = jnp.zeros((head_dim - pair_rows, head_dim), F32)
    window = lax.broadcasted_iota(jnp.int32, (16, head_dim), 0)
    nt = (((1,), (1,)), ((), ()))

    def group(i, carry):
        for cp in cache_in(i):
            cp.wait()
        for pr in range(per // 2):
            b0 = i * per + 2 * pr
            rows_at = pl.ds(pl.multiple_of(i * (per * steps) + pair_rows * pr, pair_rows), pair_rows)
            pos0 = pos_ref[b0]
            pos1 = pos_ref[b0 + 1]
            cur = jnp.where(row < steps, pos0, pos1) + step
            if slots & (slots - 1):
                dist = lax.rem(lax.rem(cur - slot, slots) + slots, slots)
            else:
                dist = (cur - slot) & (slots - 1)
            old_ok = ((dist > step) & (dist <= cur))[None]
            query = qkv[0:heads, rows_at, :].reshape(heads * pair_rows, head_dim).astype(BF16)
            new_k = jnp.concatenate([qkv[heads, rows_at, :], pad], axis=0).astype(BF16)
            new_v = jnp.concatenate([qkv[heads + 1, rows_at, :], pad], axis=0).astype(BF16)
            shape = (heads, pair_rows, local)
            score0 = lax.dot_general(query, k_buf[b0], nt, preferred_element_type=F32).reshape(shape)
            score1 = lax.dot_general(query, k_buf[b0 + 1], nt, preferred_element_type=F32).reshape(shape)
            score = jnp.where(old_ok, jnp.where((row < steps)[None], score0, score1) * scale, NEG_BIG)
            shape = (heads, pair_rows, head_dim)
            score_n = lax.dot_general(query, new_k, nt, preferred_element_type=F32).reshape(shape) * scale
            score_n = jnp.where(new_ok, score_n, NEG_BIG)
            top = jnp.max(jnp.maximum(score_n, functools.reduce(
                jnp.maximum, [score[:, :, j:j + head_dim] for j in range(0, local, head_dim)])), axis=-1, keepdims=True)
            wts = jnp.where(old_ok, jnp.exp(score - top), 0.0)
            wts_n = jnp.where(new_ok, jnp.exp(score_n - top), 0.0)
            total = jnp.sum(wts_n + sum(wts[:, :, j:j + head_dim] for j in range(0, local, head_dim)), axis=-1, keepdims=True)
            wts = wts.reshape(heads * pair_rows, local).astype(BF16)
            wts_n = wts_n.reshape(heads * pair_rows, head_dim).astype(BF16)
            out0 = jnp.dot(wts, v_buf[b0], preferred_element_type=F32).reshape(shape)
            out1 = jnp.dot(wts, v_buf[b0 + 1], preferred_element_type=F32).reshape(shape)
            out_n = jnp.dot(wts_n, new_v, preferred_element_type=F32).reshape(shape)
            out = jnp.where((n_row < steps)[None], out0, out1) + out_n
            for core in range(2):
                part_ref[core, 0:half, rows_at, :] = out[core * half:(core + 1) * half]
                stat = jnp.zeros((pair_rows, head_dim), F32)
                for h in range(half):
                    stat = jnp.where(lane == h, top[core * half + h], stat)
                    stat = jnp.where(lane == head_dim // 2 + h, total[core * half + h], stat)
                part_ref[core, half, rows_at, :] = stat
        for b in range(per):
            for t in range(steps):
                at = lax.rem(pos_ref[i * per + b] + t, slots) - first

                @pl.when((at >= 0) & (at < local))
                def _(b=b, t=t, at=at):
                    start = pl.multiple_of(lax.div(at, 16) * 16, 16)
                    hit = window == at - start
                    for src, dst in ((heads, k_buf), (heads + 1, v_buf)):
                        fresh = qkv[src, pl.ds(i * (per * steps) + b * steps + t, 1), :]
                        old = dst[i * per + b, pl.ds(start, 16), :].astype(F32)
                        dst[i * per + b, pl.ds(start, 16), :] = jnp.where(hit, fresh, old).astype(BF16)

        for cp in cache_out(i):
            cp.start()
        return carry

    lax.fori_loop(0, groups, group, 0)
    for i in range(groups):
        for cp in cache_out(i):
            cp.wait()


def merge_parts(parts, half, head_dim):
    stats = [p[half] for p in parts]
    top = functools.reduce(jnp.maximum, stats)
    scales = [jnp.exp(s - top) for s in stats]
    lane = lax.broadcasted_iota(jnp.int32, top.shape, 1)
    total = sum(s * pltpu.roll(f, head_dim // 2, 1) for s, f in zip(stats, scales))
    stat = jnp.where(lane < head_dim // 2, top, total)
    outs = []
    for h in range(half):
        outs.append(sum(p[h] * f[:, h:h + 1] for p, f in zip(parts, scales)))
    return outs, stat


def tail_kernel(part_ref, x_any, vec_ref, wo_any, wfc_any, wpj_any, y_ref,
                w_buf, x_buf, pair_in, m_part, x_in, a_own, a_in, a_full, o_part, o_in, x1_all, hid,
                g_own, g_in, g_full, p_part, p_in, y_all, w_sem, x_sem, send, recv, *, half, head_dim):
    steps, blk_b, cols = x_buf.shape
    blk = steps * blk_b
    n = 4
    width = 2 * n * cols
    core_cols = n * cols
    depth = wo_any.shape[0]
    ff = wpj_any.shape[0]
    sq = lax.axis_index("sq")
    y = lax.axis_index("tp")
    x = lax.div(sq, 2)
    c = lax.rem(sq, 2)
    mine = c * n + y
    my_col = pl.multiple_of(mine * cols, cols)
    half_col = pl.multiple_of(c * core_cols, core_cols)
    lo, hi = pl.ds(0, blk // 2), pl.ds(blk // 2, blk // 2)
    left, right = pl.ds(0, cols // 2), pl.ds(cols // 2, cols // 2)
    every = pl.ds(0, blk)
    all_cols = pl.ds(0, cols)
    partner = {"tp": y, "sq": 2 * x + 1 - c}

    def along_x(d):
        return {"tp": y, "sq": 2 * lax.rem(x + d, n) + c}

    def along_y(d):
        return {"tp": lax.rem(y + d, n), "sq": sq}

    ids = iter(range(1000))
    sent = []

    def push(src, dst, dev):
        i = next(ids)
        cp = pltpu.make_async_remote_copy(src_ref=src, dst_ref=dst, send_sem=send.at[i], recv_sem=recv.at[i],
                                          device_id=dev, device_id_type=MESH)
        cp.start()
        sent.append(cp)
        return cp

    order = (2, 1, 3, 0)

    def block_col(d):
        return pl.multiple_of(half_col + lax.rem(y + d, n) * cols, cols)

    wo_copy = [pltpu.make_async_copy(wo_any.at[:, pl.ds(block_col(d), cols)], w_buf.at[0, pl.ds(d * depth, depth)], w_sem.at[d])
               for d in range(n)]
    fc_copy = [pltpu.make_async_copy(wfc_any.at[:, pl.ds(pl.multiple_of(half_col + j * cols, cols), cols)], w_buf.at[1 + j],
                                     w_sem.at[n + j]) for j in range(n)]
    pj_copy = [pltpu.make_async_copy(wpj_any.at[:, pl.ds(block_col(d), cols)], w_buf.at[k], w_sem.at[2 * n + k])
               for k, d in enumerate(order)]
    x_copy = pltpu.make_async_copy(x_any.at[:, pl.ds(pl.multiple_of(x * blk_b, blk_b), blk_b), pl.ds(my_col, cols)], x_buf, x_sem)
    x_copy.start()
    for d in order:
        wo_copy[d].start()
    fc_copy[0].start()

    barrier = pltpu.get_barrier_semaphore()
    peers = [partner] + [along_x(d) for d in (1, 3)] + [along_y(d) for d in (1, 3)]
    for dev in peers:
        pl.semaphore_signal(barrier, inc=1, device_id=dev, device_id_type=MESH)
    pl.semaphore_wait(barrier, len(peers))

    def ring_reduce(ready, half_of, inbox, along, fold):
        ready(2)
        rel_a = push(half_of(2, lo), inbox.at[0], along(1))
        rel_b = push(half_of(2, hi), inbox.at[1], along(3))
        ready(1)
        dir_b = push(half_of(1, hi), inbox.at[2], along(1))
        ready(3)
        dir_a = push(half_of(3, lo), inbox.at[3], along(3))
        rel_a.wait_recv()
        fold(1, lo, 0)
        sum_a = push(half_of(1, lo), inbox.at[4], along(1))
        rel_b.wait_recv()
        fold(3, hi, 1)
        sum_b = push(half_of(3, hi), inbox.at[5], along(3))
        ready(0)
        for cp in (dir_b, dir_a, sum_a, sum_b):
            cp.wait_recv()

    planes = range(half + 1)
    pairs = {}
    for d in order:
        at = pl.ds(pl.multiple_of(lax.rem(x + d, n) * blk, blk), blk)
        pairs[d] = push(part_ref.at[1 - c, :, at, :], pair_in.at[d], partner)
    fc_copy[1].start()

    def pair_merge(d):
        pairs[d].wait_recv()
        at = pl.ds(pl.multiple_of(lax.rem(x + d, n) * blk, blk), blk)
        outs, stat = merge_parts([[part_ref[c, h, at, :] for h in planes], [pair_in[d, h] for h in planes]], half, head_dim)
        for h in range(half):
            m_part[d, h] = outs[h]
        m_part[d, half] = stat

    def fold_parts(d, rows, i):
        outs, stat = merge_parts([[m_part[d, h, rows, :] for h in planes], [x_in[i, h] for h in planes]], half, head_dim)
        for h in range(half):
            m_part[d, h, rows, :] = outs[h]
        m_part[d, half, rows, :] = stat

    ring_reduce(pair_merge, lambda d, rows: m_part.at[d, :, rows], x_in, along_x, fold_parts)
    for rows, terms in ((lo, (3, 4)), (hi, (2, 5))):
        parts = [[m_part[0, h, rows, :] for h in planes]] + [[x_in[i, h] for h in planes] for i in terms]
        outs, stat = merge_parts(parts, half, head_dim)
        for h in range(half):
            denom = stat[:, head_dim // 2 + h:head_dim // 2 + h + 1]
            a_own[rows, h * head_dim:(h + 1) * head_dim] = (outs[h] / denom).astype(BF16).astype(F32)
    a_copy = push(a_own, a_in, partner)
    fc_copy[2].start()
    fc_copy[3].start()
    perm = one_hot_rows(blk, steps)
    a_cols = half * head_dim
    a_full[:, pl.ds(pl.multiple_of(c * a_cols, a_cols), a_cols)] = jnp.dot(
        perm, a_own[...].astype(BF16), preferred_element_type=F32).astype(BF16)
    a_copy.wait_recv()
    a_full[:, pl.ds(pl.multiple_of((1 - c) * a_cols, a_cols), a_cols)] = jnp.dot(
        perm, a_in[...].astype(BF16), preferred_element_type=F32).astype(BF16)

    def o_block(d):
        wo_copy[d].wait()
        o_part[d] = jnp.dot(a_full[...], w_buf[0, d * depth:(d + 1) * depth, :], preferred_element_type=F32)

    def fold_o(d, rows, i):
        o_part[d, rows, :] = o_part[d, rows, :] + o_in[i]

    ring_reduce(o_block, lambda d, rows: o_part.at[d, rows], o_in, along_y, fold_o)
    pj_copy[0].start()
    x_copy.wait()
    x_own = x_buf[...].astype(F32).reshape(blk, cols) + vec_ref[0:1, pl.ds(2 * width + my_col, cols)]
    hb = blk // 2
    x1_all[mine, lo] = (x_own[:hb] + (o_part[0, lo] + (o_in[3] + o_in[4]))).astype(BF16).astype(F32)
    x1_all[mine, hi] = (x_own[hb:] + (o_part[0, hi] + (o_in[2] + o_in[5]))).astype(BF16).astype(F32)

    def x1_push(d, rows, dev):
        ref = x1_all.at[c * n + lax.rem(y + d, n), rows]
        return push(ref, ref, dev)

    p_lo = x1_push(0, lo, along_y(1))
    m_hi = x1_push(0, hi, along_y(3))
    p_hi = x1_push(0, hi, along_y(1))
    m_lo = x1_push(0, lo, along_y(3))
    fwd = [x1_push(0, every, partner)]
    p_lo.wait_recv()
    r_lo = x1_push(3, lo, along_y(1))
    m_hi.wait_recv()
    r_hi = x1_push(1, hi, along_y(3))
    p_hi.wait_recv()
    fwd.append(x1_push(3, every, partner))
    m_lo.wait_recv()
    fwd.append(x1_push(1, every, partner))
    r_lo.wait_recv()
    r_hi.wait_recv()
    fwd.append(x1_push(2, every, partner))
    for cp in fwd:
        cp.wait_recv()

    total = jnp.zeros((blk, 1), F32)
    for i in range(2 * n):
        total = total + jnp.sum(x1_all[i], axis=-1, keepdims=True)
    mean = total * (1.0 / width)
    total = jnp.zeros((blk, 1), F32)
    for i in range(2 * n):
        dev = x1_all[i] - mean
        total = total + jnp.sum(dev * dev, axis=-1, keepdims=True)
    inv = lax.rsqrt(total * (1.0 / width) + LN_EPS)
    for i in range(2 * n):
        at = slice(i * cols, (i + 1) * cols)
        gain = vec_ref[0:1, 4 * width + i * cols:4 * width + (i + 1) * cols]
        shift = vec_ref[0:1, 5 * width + i * cols:5 * width + (i + 1) * cols]
        hid[:, at] = ((x1_all[i] - mean) * inv * gain + shift).astype(BF16)

    tile = 256
    own_ff = pl.multiple_of(c * (ff // 2), ff // 2)
    g_copy = []
    for j in range(n):
        fc_copy[j].wait()

        def fc_tile(t, carry, j=j):
            at = pl.ds(pl.multiple_of(t * tile, tile), tile)
            val = jnp.dot(hid[...], w_buf[1 + j, :, at], preferred_element_type=F32)
            bias_at = pl.multiple_of(6 * width + own_ff + j * cols + t * tile, tile)
            val = val + vec_ref[0:1, pl.ds(bias_at, tile)]
            val = jax.nn.gelu(val, approximate=True).astype(BF16)
            g_own[j, :, at] = val.astype(F32)
            g_full[:, pl.ds(pl.multiple_of(own_ff + j * cols + t * tile, tile), tile)] = val
            return carry

        lax.fori_loop(0, cols // tile, fc_tile, 0)
        g_copy.append(push(g_own.at[j], g_in.at[j], partner))
        if j < n - 1:
            pj_copy[j + 1].start()
    other_ff = pl.multiple_of((1 - c) * (ff // 2), ff // 2)
    for j in range(n):
        g_copy[j].wait_recv()
        g_full[:, pl.ds(pl.multiple_of(other_ff + j * cols, cols), cols)] = g_in[j].astype(BF16)

    def p_block(d):
        k = order.index(d)
        pj_copy[k].wait()

        def pj_tile(t, carry):
            at = pl.ds(pl.multiple_of(t * tile, tile), tile)
            p_part[d, :, at] = jnp.dot(g_full[...], w_buf[k, :, at], preferred_element_type=F32)
            return carry

        lax.fori_loop(0, cols // tile, pj_tile, 0)

    def fold_p(d, rows, i):
        p_part[d, rows, :] = p_part[d, rows, :] + p_in[i]

    ring_reduce(p_block, lambda d, rows: p_part.at[d, rows], p_in, along_y, fold_p)
    bias = vec_ref[0:1, pl.ds(3 * width + my_col, cols)]
    y_all[x, mine, lo] = (x1_all[mine, lo] + (p_part[0, lo] + (p_in[3] + p_in[4])) + bias).astype(BF16).astype(F32)
    y_all[x, mine, hi] = (x1_all[mine, hi] + (p_part[0, hi] + (p_in[2] + p_in[5])) + bias).astype(BF16).astype(F32)

    def unit(dx, dy, rows=every, at=all_cols):
        return y_all.at[lax.rem(x + dx, n), c * n + lax.rem(y + dy, n), rows, at]

    def relay(dx, dy, dev, rows=every, at=all_cols):
        ref = unit(dx, dy, rows, at)
        return push(ref, ref, dev)

    fwd = []

    def forward(dx, dy):
        fwd.append(relay(dx, dy, partner))

    xp, xm, yp, ym = along_x(1), along_x(3), along_y(1), along_y(3)
    o_xp, o_xm, o_yp, o_ym = [relay(0, 0, dev) for dev in (xp, xm, yp, ym)]
    forward(0, 0)
    o_xp.wait_recv()
    r_xp = relay(3, 0, xp, at=left)
    a_yp, a_ym = relay(3, 0, yp, rows=lo), relay(3, 0, ym, rows=lo)
    o_xm.wait_recv()
    r_xm = relay(1, 0, xm, at=right)
    b_yp, b_ym = relay(1, 0, yp, rows=lo), relay(1, 0, ym, rows=lo)
    o_yp.wait_recv()
    r_yp = relay(0, 3, yp, at=left)
    a_xp, a_xm = relay(0, 3, xp, rows=hi), relay(0, 3, xm, rows=hi)
    o_ym.wait_recv()
    r_ym = relay(0, 1, ym, at=right)
    b_xp, b_xm = relay(0, 1, xp, rows=hi), relay(0, 1, xm, rows=hi)
    for d in ((3, 0), (1, 0), (0, 3), (0, 1)):
        forward(*d)
    r_xp.wait_recv()
    c_yp, c_ym = relay(2, 0, yp, lo, left), relay(2, 0, ym, lo, left)
    r_xm.wait_recv()
    d_yp, d_ym = relay(2, 0, yp, lo, right), relay(2, 0, ym, lo, right)
    r_yp.wait_recv()
    c_xp, c_xm = relay(0, 2, xp, hi, left), relay(0, 2, xm, hi, left)
    r_ym.wait_recv()
    d_xp, d_xm = relay(0, 2, xp, hi, right), relay(0, 2, xm, hi, right)
    forward(2, 0)
    forward(0, 2)
    late = []
    for cp, dx, dy, dev, rows, at in ((a_yp, 3, 3, yp, lo, left), (a_ym, 3, 1, ym, lo, right),
                                      (b_yp, 1, 3, yp, lo, left), (b_ym, 1, 1, ym, lo, right),
                                      (a_xp, 3, 3, xp, hi, left), (a_xm, 1, 3, xm, hi, right),
                                      (b_xp, 3, 1, xp, hi, left), (b_xm, 1, 1, xm, hi, right)):
        cp.wait_recv()
        late.append(relay(dx, dy, dev, rows, at))
    for d in ((3, 3), (3, 1), (1, 3), (1, 1)):
        forward(*d)
    for cp, dx, dy, dev, rows, at in ((c_yp, 2, 3, yp, lo, left), (d_ym, 2, 1, ym, lo, right),
                                      (c_xp, 3, 2, xp, hi, left), (d_xm, 1, 2, xm, hi, right)):
        cp.wait_recv()
        late.append(relay(dx, dy, dev, rows, at))
    for cp in (c_ym, d_yp, c_xm, d_xp):
        cp.wait_recv()
    for cp in late[:8]:
        cp.wait_recv()
    for d in ((3, 2), (1, 2), (2, 3), (2, 1)):
        forward(*d)
    for cp in late[8:]:
        cp.wait_recv()
    forward(2, 2)
    for cp in fwd:
        cp.wait_recv()
    for s in range(steps):
        for xb in range(0, n, 2):
            for i in range(2 * n):
                block = jnp.concatenate([y_all[xb, i, s * blk_b:(s + 1) * blk_b, :],
                                         y_all[xb + 1, i, s * blk_b:(s + 1) * blk_b, :]], axis=0)
                y_ref[s, xb * blk_b:(xb + 2) * blk_b, i * cols:(i + 1) * cols] = block.astype(BF16)
    for cp in sent:
        cp.wait_send()


def solution(mesh):
    n_sq = mesh.shape["sq"]
    n_y = mesh.shape["tp"]
    n_x = n_sq // 2
    act_spec = P(None, "dp", None)
    cache_spec = P("dp", "sq", "tp", None)
    col_spec = P(None, "tp")
    row_spec = P("tp", None)
    vec_spec = P("tp")
    rep_spec = P(None)
    in_specs = (act_spec, P("dp"), cache_spec, cache_spec, col_spec, vec_spec, col_spec, vec_spec,
                col_spec, vec_spec, row_spec, rep_spec, rep_spec, rep_spec, rep_spec, rep_spec,
                col_spec, vec_spec, row_spec, rep_spec)
    out_specs = (act_spec, cache_spec, cache_spec)
    vmem = pl.BlockSpec(memory_space=pltpu.VMEM)
    hbm = pl.BlockSpec(memory_space=pl.ANY)

    def per_device(x_steps, positions, key_buf, val_buf, w_q, b_q, w_k, b_k, w_v, b_v, w_o, b_o,
                   ln1_gain, ln1_bias, ln2_gain, ln2_bias, w_fc, b_fc, w_proj, b_proj):
        steps, batch, width = x_steps.shape
        local, head_dim = key_buf.shape[1], key_buf.shape[3]
        rows = steps * batch
        heads = w_q.shape[1] // head_dim
        half = heads // 2
        vecs = jnp.concatenate([v.astype(F32) for v in (ln1_gain, ln1_bias, b_o, b_proj, ln2_gain, ln2_bias,
                                                        b_fc, b_q, b_k, b_v)]).reshape(1, -1)
        half_dim = head_dim // 2
        inv_freq = jnp.power(jnp.float32(ROPE_BASE), -2.0 * jnp.arange(half_dim, dtype=F32) / head_dim)
        inv_freq = jnp.concatenate([inv_freq, inv_freq])[None, None, :]
        sign = jnp.where(jnp.arange(head_dim) < half_dim, -1.0, 1.0).astype(F32)
        cur = positions[None, :, None] + jnp.arange(steps, dtype=jnp.int32)[:, None, None]
        angle = cur.astype(F32) * inv_freq
        cos_t = jnp.cos(angle).reshape(rows, head_dim)
        sin_t = (jnp.sin(angle) * sign).reshape(rows, head_dim)

        per, bands = 4, 6
        groups = batch // per
        smem = pl.BlockSpec(memory_space=pltpu.SMEM)
        part, k_new, v_new = pl.pallas_call(
            functools.partial(front_kernel, batch=batch, heads=heads, head_dim=head_dim, steps=steps, per=per),
            out_shape=(jax.ShapeDtypeStruct((2, half + 1, rows, head_dim), F32),
                       jax.ShapeDtypeStruct((batch, local, head_dim), BF16),
                       jax.ShapeDtypeStruct((batch, local, head_dim), BF16)),
            in_specs=[smem, hbm, hbm, hbm, hbm, vmem, vmem, vmem, hbm, hbm],
            out_specs=(vmem, hbm, hbm),
            scratch_shapes=[
                pltpu.VMEM((rows, width), BF16),
                pltpu.VMEM((rows, width), BF16),
                pltpu.VMEM((bands, width // bands, heads * head_dim), BF16),
                pltpu.VMEM((width, head_dim), BF16),
                pltpu.VMEM((width, head_dim), BF16),
                pltpu.VMEM((rows, heads * head_dim), F32),
                pltpu.VMEM((heads + 2, rows, head_dim), F32),
                pltpu.VMEM((batch, local, head_dim), BF16),
                pltpu.VMEM((batch, local, head_dim), BF16),
                pltpu.SemaphoreType.DMA,
                pltpu.SemaphoreType.DMA((bands,)),
                pltpu.SemaphoreType.DMA((2,)),
                pltpu.SemaphoreType.DMA((2, groups)),
                pltpu.SemaphoreType.DMA((2, groups)),
            ],
            compiler_params=pltpu.CompilerParams(vmem_limit_bytes=VMEM_BYTES),
            name="front",
        )(positions, x_steps.reshape(rows, width), w_q, w_k, w_v, vecs, cos_t, sin_t,
          key_buf.reshape(batch, local, head_dim), val_buf.reshape(batch, local, head_dim))

        cols = width // (2 * n_y)
        core_cols = width // 2
        blk_b = batch // n_x
        blk = blk_b * steps
        ys = pl.pallas_call(
            functools.partial(tail_kernel, half=half, head_dim=head_dim),
            out_shape=jax.ShapeDtypeStruct((steps, batch, width), BF16),
            in_specs=[vmem, hbm, vmem, hbm, hbm, hbm],
            out_specs=vmem,
            scratch_shapes=[
                pltpu.VMEM((5, width, cols), BF16),
                pltpu.VMEM((steps, blk_b, cols), BF16),
                pltpu.VMEM((4, half + 1, blk, head_dim), F32),
                pltpu.VMEM((4, half + 1, blk, head_dim), F32),
                pltpu.VMEM((6, half + 1, blk // 2, head_dim), F32),
                pltpu.VMEM((blk, half * head_dim), F32),
                pltpu.VMEM((blk, half * head_dim), F32),
                pltpu.VMEM((blk, heads * head_dim), BF16),
                pltpu.VMEM((4, blk, cols), F32),
                pltpu.VMEM((6, blk // 2, cols), F32),
                pltpu.VMEM((8, blk, cols), F32),
                pltpu.VMEM((blk, width), BF16),
                pltpu.VMEM((4, blk, cols), F32),
                pltpu.VMEM((4, blk, cols), F32),
                pltpu.VMEM((blk, w_proj.shape[0]), BF16),
                pltpu.VMEM((4, blk, cols), F32),
                pltpu.VMEM((6, blk // 2, cols), F32),
                pltpu.VMEM((4, 8, blk, cols), F32),
                pltpu.SemaphoreType.DMA((12,)),
                pltpu.SemaphoreType.DMA,
                pltpu.SemaphoreType.DMA((100,)),
                pltpu.SemaphoreType.DMA((100,)),
            ],
            compiler_params=pltpu.CompilerParams(collective_id=0, has_side_effects=True, vmem_limit_bytes=VMEM_BYTES),
            name="tail",
        )(part, x_steps, vecs, w_o, w_fc, w_proj)
        return ys, k_new.reshape(key_buf.shape), v_new.reshape(val_buf.shape)

    return jax.shard_map(per_device, mesh=mesh, in_specs=in_specs, out_specs=out_specs, check_vma=False)
```

time: 597 us -> 120 us (0.20); the launches traced: 589 us -> 119 us
  matrix products: 320 us -> 0 us
  waiting for transfers between devices: 149 us -> 0 us
  Pallas kernels: 0 us -> 106 us
  local copies, waits for them, and re-layouts: 68.3 us -> 11.8 us
  other arithmetic: 34 us -> 1.05 us
  between operations: 15.7 us -> 0.66 us
    dot_general x32 -> x0, matrix products: 320 us -> none  [the longest x16 159 us: linear(): jnp.dot(rows_in, weight, preferred_element_type=jnp.float32)]
    psum x2 -> x0, waiting for transfers between devices: 139 us -> none  [the longest x1 69.5 us: layer_tail(): lax.psum(jnp.dot(attn_out, w_o, preferred_element_type=jnp.float32), 'tp')]
    pallas_call x0 -> x2, Pallas kernels: none -> 106 us  [the longest x1 74.8 us: per_device(): pl.pallas_call(functools.partial(tail_kernel, half=half, head_dim=head_di...]
    scatter x8 -> x0, local copies, waits for them, and re-layouts: 35.4 us -> none  [the longest x4 17.7 us: per_device(): val_buf = val_buf.at[batch_ids, local_slot].set(v_heads, mode='drop')]
    all_gather x4 -> x0, local copies, waits for them, and re-layouts: 13.6 us -> none  [per_device(): gathered = lax.all_gather(stats, 'sq')]
    reduce_sum x19 -> x0, other arithmetic: 10.6 us -> none  [the longest x2 4 us: layer_norm(): row_mean = jnp.mean(vectors, axis=-1, keepdims=True)]
    all_gather x4 -> x0, waiting for transfers between devices: 10.2 us -> none  [per_device(): gathered = lax.all_gather(stats, 'sq')]
    slice x4 -> x0, other arithmetic: 7.62 us -> none  [per_device(): all_max = gathered[..., head_dim + 1]]
  transfers between devices with their start and end apart: 6 -> 0, of which waited for: 3 -> 0; matrix products, arithmetic and copies ran while one was open for 19% -> 0% of each run, Pallas kernels for 0% -> 0%
where the time goes in v2:
time: 120 us; the launch traced here: 119 us
  Pallas kernels  106 us (88%)
  local copies, waits for them, and re-layouts  11.8 us (10%)
    pallas_call x1, Pallas kernels, per_device(): pl.pallas_call(functools.partial(tail_kernel, half=half, head_dim=head_di...  74.8 us
    pallas_call x1, Pallas kernels, per_device(): pl.pallas_call(functools.partial(front_kernel, batch=batch, heads=heads,...  30.8 us
    unnamed x10, local copies, waits for them, and re-layouts  9.33 us

profile of v2, /device:TPU:97, one launch (start us, length us, event | category | flops | bytes accessed | tf_op | source)
XLA Modules:
  0.0 119.1 jit_solution(9427931031661871003)
XLA Ops:
  0.6 0.1 compare_select_fusion
  0.7 0.7 add.22
  1.4 0.1 add.23
  1.5 0.1 add.25
  1.6 0.7 constant_dynamic-update-slice_fusion.6
  2.3 0.7 constant_dynamic-update-slice_fusion.5
  3.0 0.7 constant_dynamic-update-slice_fusion.4
  3.7 0.7 constant_dynamic-update-slice_fusion.3
  4.4 0.7 constant_dynamic-update-slice_fusion.2
  5.1 0.7 constant_dynamic-update-slice_fusion.1
  5.8 0.7 constant_dynamic-update-slice_fusion
  6.5 0.9 dynamic-update-slice.7
  7.4 0.8 dynamic-update-slice.8
  8.2 0.8 dynamic-update-slice.9
  9.0 0.8 reshape.69.vec_ref
  9.8 1.0 fusion
  10.8 30.8 %front.1 = (f32[2,7,128,128]{3,2,1,0:T(8,128)}, bf16[32,512,128]{2,1,0:T(8,128)(2,1)}, bf16[32,512,128]{2,1,0:T(8,128)(2,1)}) custom-call(s32[32]{0:T(128)} %pos_ref.1, bf16[128,6144]{1,0:T(8,128)(2,1)} %bitcast.11, bf16[6144,1536]{1,0:T(8,128)(2,1)} %wq_any.1, bf16[6144,128]{1,0:T(8,128)(2,1)} %wk_any.1, bf16[6144,128]{1,0:T(8,128)(2,1)} %wv_any.1, ...), custom_call_target="tpu_custom_call" | custom-call | tf_op jit(solution)/shard_map/front/pallas_call | solution.py:535
  41.6 74.8 %tail.1 = bf16[4,32,6144]{2,1,0:T(8,128)(2,1)} custom-call(f32[2,7,128,128]{3,2,1,0:T(8,128)} %get-tuple-element.6.part_ref, bf16[4,32,6144]{2,1,0:T(8,128)(2,1)} %x_any.1, f32[1,44800]{1,0:T(1,128)} %reshape.69.vec_ref, bf16[1536,6144]{1,0:T(8,128)(2,1)} %wo_any.1, bf16[6144,6144]{1,0:T(8,128)(2,1)} %wfc_any.1, bf16[6144,6144]{1,0:T(8,128)(2,1)} %wpj_any.1), custom_call_target="tpu_custom_call" | custom-call | tf_op jit(solution)/shard_map/tail/pallas_call | solution.py:567
  116.4 2.7 %copy.35 = bf16[4,32,6144]{2,1,0:T(8,128)(2,1)} copy(bf16[4,32,6144]{2,1,0:T(8,128)(2,1)} %tail.1) | data formatting | bytes 3145728
  (3 shorter events, 0.0 us)

commit v3 on v2

--- a/solution.py
+++ b/solution.py
@@ -24,7 +24,8 @@
     return jnp.where(col == source, 1.0, 0.0).astype(BF16)
 
 
-def front_kernel(pos_ref, x_any, wq_any, wk_any, wv_any, vec_ref, cos_ref, sin_ref, kc_any, vc_any,
+def front_kernel(pos_ref, x_any, wq_any, wk_any, wv_any, gain_ref, shift_ref, bq_ref, bk_ref, bv_ref, cos_ref, sin_ref,
+                 kc_any, vc_any,
                  part_ref, kout_any, vout_any,
                  x_buf, hid, wq_buf, wk_buf, wv_buf, acc, qkv, k_buf, v_buf,
                  x_sem, wq_sem, kv_sem, c_sem, out_sem, *, batch, heads, head_dim, steps, per):
@@ -42,8 +43,6 @@
     x_copy.start()
     k_copy = pltpu.make_async_copy(wk_any, wk_buf, kv_sem.at[0])
     v_copy = pltpu.make_async_copy(wv_any, wv_buf, kv_sem.at[1])
-    k_copy.start()
-    v_copy.start()
 
     def q_copy(i):
         return pltpu.make_async_copy(wq_any.at[pl.ds(pl.multiple_of(i * band, band), band), :], wq_buf.at[i], wq_sem.at[i])
@@ -58,15 +57,13 @@
         return (pltpu.make_async_copy(k_buf.at[at], kout_any.at[at], out_sem.at[0, i]),
                 pltpu.make_async_copy(v_buf.at[at], vout_any.at[at], out_sem.at[1, i]))
 
-    for i in range(bands):
+    gain = as_row(gain_ref)
+    shift = as_row(shift_ref)
+    x_copy.wait()
+    k_copy.start()
+    v_copy.start()
+    for i in range(bands // 2):
         q_copy(i).start()
-    for i in range(groups):
-        for cp in cache_in(i):
-            cp.start()
-
-    gain = vec_ref[0:1, 0:width]
-    shift = vec_ref[0:1, width:2 * width]
-    x_copy.wait()
 
     def norm_rows(i, carry):
         at = pl.ds(pl.multiple_of(i * 16, 16), 16)
@@ -77,9 +74,8 @@
         hid[at, :] = (vals * lax.rsqrt(var + LN_EPS) * gain + shift).astype(BF16)
         return carry
 
-    lax.fori_loop(0, rows // 16, norm_rows, 0)
-
-    bias0 = vec_ref.shape[1] - n_q - 2 * head_dim
+    lax.fori_loop(0, rows // 16, norm_rows, 0, unroll=2)
+
     perm = one_hot_rows(rows, batch)
     cos_t = cos_ref[...]
     sin_t = sin_ref[...]
@@ -92,25 +88,31 @@
 
     k_copy.wait()
     v_copy.wait()
-    k_new = jnp.dot(hid[...], wk_buf[...], preferred_element_type=F32) + vec_ref[0:1, bias0 + n_q:bias0 + n_q + head_dim]
-    v_new = jnp.dot(hid[...], wv_buf[...], preferred_element_type=F32) + vec_ref[0:1, bias0 + n_q + head_dim:]
+    for i in range(bands // 2, bands):
+        q_copy(i).start()
+    k_new = jnp.dot(hid[...], wk_buf[...], preferred_element_type=F32) + as_row(bk_ref)
+    v_new = jnp.dot(hid[...], wv_buf[...], preferred_element_type=F32) + as_row(bv_ref)
     qkv[heads] = by_batch(rotate(k_new.astype(BF16).astype(F32)))
     qkv[heads + 1] = by_batch(v_new)
-    acc[...] = jnp.broadcast_to(vec_ref[0:1, bias0:bias0 + n_q], acc.shape)
+    acc[...] = jnp.broadcast_to(as_row(bq_ref), acc.shape)
 
     def q_band(i, carry):
         q_copy(i).wait()
+
+        @pl.when(i >= bands - groups // 2)
+        def _():
+            for j in range(2):
+                for cp in cache_in(2 * (i - bands + groups // 2) + j):
+                    cp.start()
+
         acc[...] += jnp.dot(hid[:, pl.ds(pl.multiple_of(i * band, band), band)], wq_buf[i], preferred_element_type=F32)
         return carry
 
     lax.fori_loop(0, bands, q_band, 0)
 
-    def q_head(h, carry):
-        vals = acc[:, pl.ds(pl.multiple_of(h * head_dim, head_dim), head_dim)]
+    for h in range(heads):
+        vals = acc[:, h * head_dim:(h + 1) * head_dim]
         qkv[h] = by_batch(rotate(vals.astype(BF16).astype(F32)))
-        return carry
-
-    lax.fori_loop(0, heads, q_head, 0)
 
     scale = head_dim ** -0.5
     pair_rows = 2 * steps
@@ -169,17 +171,22 @@
                     stat = jnp.where(lane == head_dim // 2 + h, total[core * half + h], stat)
                 part_ref[core, half, rows_at, :] = stat
         for b in range(per):
-            for t in range(steps):
-                at = lax.rem(pos_ref[i * per + b] + t, slots) - first
-
-                @pl.when((at >= 0) & (at < local))
-                def _(b=b, t=t, at=at):
-                    start = pl.multiple_of(lax.div(at, 16) * 16, 16)
-                    hit = window == at - start
-                    for src, dst in ((heads, k_buf), (heads + 1, v_buf)):
-                        fresh = qkv[src, pl.ds(i * (per * steps) + b * steps + t, 1), :]
-                        old = dst[i * per + b, pl.ds(start, 16), :].astype(F32)
-                        dst[i * per + b, pl.ds(start, 16), :] = jnp.where(hit, fresh, old).astype(BF16)
+            lead = pos_ref[i * per + b] - first
+            head_at = lax.rem(lead + slots, slots)
+
+            @pl.when((head_at < local) | (head_at >= slots - steps))
+            def _(b=b, head_at=head_at):
+                for t in range(steps):
+                    at = lax.rem(head_at + t, slots)
+
+                    @pl.when(at < local)
+                    def _(t=t, at=at):
+                        start = pl.multiple_of(lax.div(at, 16) * 16, 16)
+                        hit = window == at - start
+                        for src, dst in ((heads, k_buf), (heads + 1, v_buf)):
+                            fresh = qkv[src, pl.ds(i * (per * steps) + b * steps + t, 1), :]
+                            old = dst[i * per + b, pl.ds(start, 16), :].astype(F32)
+                            dst[i * per + b, pl.ds(start, 16), :] = jnp.where(hit, fresh, old).astype(BF16)
 
         for cp in cache_out(i):
             cp.start()
@@ -189,6 +196,10 @@
     for i in range(groups):
         for cp in cache_out(i):
             cp.wait()
+
+
+def as_row(ref):
+    return ref[...].astype(F32).reshape(1, ref.shape[0])
 
 
 def merge_parts(parts, half, head_dim):
@@ -204,9 +215,9 @@
     return outs, stat
 
 
-def tail_kernel(part_ref, x_any, vec_ref, wo_any, wfc_any, wpj_any, y_ref,
+def tail_kernel(part_ref, x_any, bo_ref, bpj_ref, gain_ref, shift_ref, bfc_ref, wo_any, wfc_any, wpj_any, y_ref,
                 w_buf, x_buf, pair_in, m_part, x_in, a_own, a_in, a_full, o_part, o_in, x1_all, hid,
-                g_own, g_in, g_full, p_part, p_in, y_all, w_sem, x_sem, send, recv, *, half, head_dim):
+                g_own, g_in, g_full, p_part, p_in, y_all, bias_rows, w_sem, x_sem, send, recv, *, half, head_dim):
     steps, blk_b, cols = x_buf.shape
     blk = steps * blk_b
     n = 4
@@ -265,6 +276,8 @@
     peers = [partner] + [along_x(d) for d in (1, 3)] + [along_y(d) for d in (1, 3)]
     for dev in peers:
         pl.semaphore_signal(barrier, inc=1, device_id=dev, device_id_type=MESH)
+    for i, ref in enumerate((bo_ref, bpj_ref, bfc_ref, gain_ref, shift_ref)):
+        bias_rows[8 * i:8 * i + 1, :] = as_row(ref)
     pl.semaphore_wait(barrier, len(peers))
 
     def ring_reduce(ready, half_of, inbox, along, fold):
@@ -334,7 +347,7 @@
     ring_reduce(o_block, lambda d, rows: o_part.at[d, rows], o_in, along_y, fold_o)
     pj_copy[0].start()
     x_copy.wait()
-    x_own = x_buf[...].astype(F32).reshape(blk, cols) + vec_ref[0:1, pl.ds(2 * width + my_col, cols)]
+    x_own = x_buf[...].astype(F32).reshape(blk, cols) + bias_rows[0:1, pl.ds(my_col, cols)]
     hb = blk // 2
     x1_all[mine, lo] = (x_own[:hb] + (o_part[0, lo] + (o_in[3] + o_in[4]))).astype(BF16).astype(F32)
     x1_all[mine, hi] = (x_own[hb:] + (o_part[0, hi] + (o_in[2] + o_in[5]))).astype(BF16).astype(F32)
@@ -373,27 +386,20 @@
     inv = lax.rsqrt(total * (1.0 / width) + LN_EPS)
     for i in range(2 * n):
         at = slice(i * cols, (i + 1) * cols)
-        gain = vec_ref[0:1, 4 * width + i * cols:4 * width + (i + 1) * cols]
-        shift = vec_ref[0:1, 5 * width + i * cols:5 * width + (i + 1) * cols]
+        gain = bias_rows[24:25, at]
+        shift = bias_rows[32:33, at]
         hid[:, at] = ((x1_all[i] - mean) * inv * gain + shift).astype(BF16)
 
-    tile = 256
     own_ff = pl.multiple_of(c * (ff // 2), ff // 2)
     g_copy = []
     for j in range(n):
         fc_copy[j].wait()
 
-        def fc_tile(t, carry, j=j):
-            at = pl.ds(pl.multiple_of(t * tile, tile), tile)
-            val = jnp.dot(hid[...], w_buf[1 + j, :, at], preferred_element_type=F32)
-            bias_at = pl.multiple_of(6 * width + own_ff + j * cols + t * tile, tile)
-            val = val + vec_ref[0:1, pl.ds(bias_at, tile)]
-            val = jax.nn.gelu(val, approximate=True).astype(BF16)
-            g_own[j, :, at] = val.astype(F32)
-            g_full[:, pl.ds(pl.multiple_of(own_ff + j * cols + t * tile, tile), tile)] = val
-            return carry
-
-        lax.fori_loop(0, cols // tile, fc_tile, 0)
+        val = jnp.dot(hid[...], w_buf[1 + j], preferred_element_type=F32)
+        ff_at = pl.ds(pl.multiple_of(own_ff + j * cols, cols), cols)
+        val = jax.nn.gelu(val + bias_rows[16:17, ff_at], approximate=True).astype(BF16)
+        g_own[j] = val.astype(F32)
+        g_full[:, ff_at] = val
         g_copy.append(push(g_own.at[j], g_in.at[j], partner))
         if j < n - 1:
             pj_copy[j + 1].start()
@@ -406,18 +412,13 @@
         k = order.index(d)
         pj_copy[k].wait()
 
-        def pj_tile(t, carry):
-            at = pl.ds(pl.multiple_of(t * tile, tile), tile)
-            p_part[d, :, at] = jnp.dot(g_full[...], w_buf[k, :, at], preferred_element_type=F32)
-            return carry
-
-        lax.fori_loop(0, cols // tile, pj_tile, 0)
+        p_part[d] = jnp.dot(g_full[...], w_buf[k], preferred_element_type=F32)
 
     def fold_p(d, rows, i):
         p_part[d, rows, :] = p_part[d, rows, :] + p_in[i]
 
     ring_reduce(p_block, lambda d, rows: p_part.at[d, rows], p_in, along_y, fold_p)
-    bias = vec_ref[0:1, pl.ds(3 * width + my_col, cols)]
+    bias = bias_rows[8:9, pl.ds(my_col, cols)]
     y_all[x, mine, lo] = (x1_all[mine, lo] + (p_part[0, lo] + (p_in[3] + p_in[4])) + bias).astype(BF16).astype(F32)
     y_all[x, mine, hi] = (x1_all[mine, hi] + (p_part[0, hi] + (p_in[2] + p_in[5])) + bias).astype(BF16).astype(F32)
 
@@ -434,19 +435,26 @@
         fwd.append(relay(dx, dy, partner))
 
     xp, xm, yp, ym = along_x(1), along_x(3), along_y(1), along_y(3)
-    o_xp, o_xm, o_yp, o_ym = [relay(0, 0, dev) for dev in (xp, xm, yp, ym)]
+    own = {}
+    for first_half in (True, False):
+        for key, dev in (("xp", xp), ("xm", xm), ("yp", yp), ("ym", ym)):
+            own[key, first_half] = relay(0, 0, dev, at=left if (key[1] == "p") == first_half else right)
     forward(0, 0)
-    o_xp.wait_recv()
+    own["xp", True].wait_recv()
     r_xp = relay(3, 0, xp, at=left)
+    own["xm", True].wait_recv()
+    r_xm = relay(1, 0, xm, at=right)
+    own["yp", True].wait_recv()
+    r_yp = relay(0, 3, yp, at=left)
+    own["ym", True].wait_recv()
+    r_ym = relay(0, 1, ym, at=right)
+    own["xp", False].wait_recv()
     a_yp, a_ym = relay(3, 0, yp, rows=lo), relay(3, 0, ym, rows=lo)
-    o_xm.wait_recv()
-    r_xm = relay(1, 0, xm, at=right)
+    own["xm", False].wait_recv()
     b_yp, b_ym = relay(1, 0, yp, rows=lo), relay(1, 0, ym, rows=lo)
-    o_yp.wait_recv()
-    r_yp = relay(0, 3, yp, at=left)
+    own["yp", False].wait_recv()
     a_xp, a_xm = relay(0, 3, xp, rows=hi), relay(0, 3, xm, rows=hi)
-    o_ym.wait_recv()
-    r_ym = relay(0, 1, ym, at=right)
+    own["ym", False].wait_recv()
     b_xp, b_xm = relay(0, 1, xp, rows=hi), relay(0, 1, xm, rows=hi)
     for d in ((3, 0), (1, 0), (0, 3), (0, 1)):
         forward(*d)
@@ -518,8 +526,6 @@
         rows = steps * batch
         heads = w_q.shape[1] // head_dim
         half = heads // 2
-        vecs = jnp.concatenate([v.astype(F32) for v in (ln1_gain, ln1_bias, b_o, b_proj, ln2_gain, ln2_bias,
-                                                        b_fc, b_q, b_k, b_v)]).reshape(1, -1)
         half_dim = head_dim // 2
         inv_freq = jnp.power(jnp.float32(ROPE_BASE), -2.0 * jnp.arange(half_dim, dtype=F32) / head_dim)
         inv_freq = jnp.concatenate([inv_freq, inv_freq])[None, None, :]
@@ -537,7 +543,7 @@
             out_shape=(jax.ShapeDtypeStruct((2, half + 1, rows, head_dim), F32),
                        jax.ShapeDtypeStruct((batch, local, head_dim), BF16),
                        jax.ShapeDtypeStruct((batch, local, head_dim), BF16)),
-            in_specs=[smem, hbm, hbm, hbm, hbm, vmem, vmem, vmem, hbm, hbm],
+            in_specs=[smem] + [hbm] * 4 + [vmem] * 7 + [hbm] * 2,
             out_specs=(vmem, hbm, hbm),
             scratch_shapes=[
                 pltpu.VMEM((rows, width), BF16),
@@ -557,7 +563,7 @@
             ],
             compiler_params=pltpu.CompilerParams(vmem_limit_bytes=VMEM_BYTES),
             name="front",
-        )(positions, x_steps.reshape(rows, width), w_q, w_k, w_v, vecs, cos_t, sin_t,
+        )(positions, x_steps.reshape(rows, width), w_q, w_k, w_v, ln1_gain, ln1_bias, b_q, b_k, b_v, cos_t, sin_t,
           key_buf.reshape(batch, local, head_dim), val_buf.reshape(batch, local, head_dim))
 
         cols = width // (2 * n_y)
@@ -567,7 +573,7 @@
         ys = pl.pallas_call(
             functools.partial(tail_kernel, half=half, head_dim=head_dim),
             out_shape=jax.ShapeDtypeStruct((steps, batch, width), BF16),
-            in_specs=[vmem, hbm, vmem, hbm, hbm, hbm],
+            in_specs=[vmem, hbm] + [vmem] * 5 + [hbm] * 3,
             out_specs=vmem,
             scratch_shapes=[
                 pltpu.VMEM((5, width, cols), BF16),
@@ -588,6 +594,7 @@
                 pltpu.VMEM((4, blk, cols), F32),
                 pltpu.VMEM((6, blk // 2, cols), F32),
                 pltpu.VMEM((4, 8, blk, cols), F32),
+                pltpu.VMEM((40, width), F32),
                 pltpu.SemaphoreType.DMA((12,)),
                 pltpu.SemaphoreType.DMA,
                 pltpu.SemaphoreType.DMA((100,)),
@@ -595,7 +602,7 @@
             ],
             compiler_params=pltpu.CompilerParams(collective_id=0, has_side_effects=True, vmem_limit_bytes=VMEM_BYTES),
             name="tail",
-        )(part, x_steps, vecs, w_o, w_fc, w_proj)
+        )(part, x_steps, b_o, b_proj, ln2_gain, ln2_bias, b_fc, w_o, w_fc, w_proj)
         return ys, k_new.reshape(key_buf.shape), v_new.reshape(val_buf.shape)
 
     return jax.shard_map(per_device, mesh=mesh, in_specs=in_specs, out_specs=out_specs, check_vma=False)

time: 120 us -> 98.6 us (0.82)
  Pallas kernels: 106 us -> 92.7 us
  local copies, waits for them, and re-layouts: 11.8 us -> 3.52 us
    pallas_call x1, Pallas kernels: 30.8 us -> 21.1 us  [per_device(): pl.pallas_call(functools.partial(front_kernel, batch=batch, heads=heads,...]
    unnamed x10 -> x1, local copies, waits for them, and re-layouts: 9.33 us -> 2.69 us
    pallas_call x1, Pallas kernels: 74.8 us -> 71.6 us  [per_device(): pl.pallas_call(functools.partial(tail_kernel, half=half, head_dim=head_di...]
where the time goes in v3:
time: 98.6 us; the launch traced here: 97.9 us
  Pallas kernels  92.7 us (94%)
  local copies, waits for them, and re-layouts  3.52 us (4%)
  other arithmetic  1.05 us (1%)
    pallas_call x1, Pallas kernels, per_device(): pl.pallas_call(functools.partial(tail_kernel, half=half, head_dim=head_di...  71.6 us
    pallas_call x1, Pallas kernels, per_device(): pl.pallas_call(functools.partial(front_kernel, batch=batch, heads=heads,...  21.1 us
    unnamed x1, local copies, waits for them, and re-layouts  2.69 us

profile of v3, /device:TPU:97, one launch (start us, length us, event | category | flops | bytes accessed | tf_op | source)
XLA Modules:
  0.0 97.9 jit_solution(1134007204306934536)
XLA Ops:
  0.6 0.1 compare_select_fusion
  0.7 0.7 add.22
  1.4 0.1 add.23
  1.5 0.1 add.25
  1.6 1.0 fusion
  2.5 21.1 %front.1 = (f32[2,7,128,128]{3,2,1,0:T(8,128)}, bf16[32,512,128]{2,1,0:T(8,128)(2,1)}, bf16[32,512,128]{2,1,0:T(8,128)(2,1)}) custom-call(s32[32]{0:T(128)} %pos_ref.1, bf16[128,6144]{1,0:T(8,128)(2,1)} %bitcast.11, bf16[6144,1536]{1,0:T(8,128)(2,1)} %wq_any.1, bf16[6144,128]{1,0:T(8,128)(2,1)} %wk_any.1, bf16[6144,128]{1,0:T(8,128)(2,1)} %wv_any.1, ...), custom_call_target="tpu_custom_call" | custom-call | tf_op jit(solution)/shard_map/front/pallas_call | solution.py:541
  23.6 71.6 %tail.1 = bf16[4,32,6144]{2,1,0:T(8,128)(2,1)} custom-call(f32[2,7,128,128]{3,2,1,0:T(8,128)} %get-tuple-element.6.part_ref, bf16[4,32,6144]{2,1,0:T(8,128)(2,1)} %x_any.1, bf16[6144]{0:T(1024)(128)(2,1)} %bo_ref.1, bf16[6144]{0:T(1024)(128)(2,1)} %bpj_ref.1, bf16[6144]{0:T(1024)(128)(2,1)} %gain_ref.3, bf16[6144]{0:T(1024)(128)(2,1)} %shift_ref.3, ...), custom_call_target="tpu_custom_call" | custom-call | tf_op jit(solution)/shard_map/tail/pallas_call | solution.py:573
  95.2 2.7 %copy.26 = bf16[4,32,6144]{2,1,0:T(8,128)(2,1)} copy(bf16[4,32,6144]{2,1,0:T(8,128)(2,1)} %tail.1) | data formatting | bytes 3145728
  (3 shorter events, 0.0 us)

commit v4 on v3

--- a/solution.py
+++ b/solution.py
@@ -27,7 +27,7 @@
 def front_kernel(pos_ref, x_any, wq_any, wk_any, wv_any, gain_ref, shift_ref, bq_ref, bk_ref, bv_ref, cos_ref, sin_ref,
                  kc_any, vc_any,
                  part_ref, kout_any, vout_any,
-                 x_buf, hid, wq_buf, wk_buf, wv_buf, acc, qkv, k_buf, v_buf,
+                 x_buf, hid, wq_buf, wk_buf, wv_buf, acc, qkv, k_buf, v_buf, s_buf, n_buf, p_buf,
                  x_sem, wq_sem, kv_sem, c_sem, out_sem, *, batch, heads, head_dim, steps, per):
     rows, width = x_buf.shape
     n_q = heads * head_dim
@@ -39,8 +39,12 @@
     first = lax.axis_index("sq") * local
     leader = lax.axis_index("sq") == 0
 
-    x_copy = pltpu.make_async_copy(x_any, x_buf, x_sem)
-    x_copy.start()
+    def x_copy(i):
+        at = pl.ds(pl.multiple_of(i * 16, 16), 16)
+        return pltpu.make_async_copy(x_any.at[at], x_buf.at[at], x_sem.at[i])
+
+    for i in range(rows // 16):
+        x_copy(i).start()
     k_copy = pltpu.make_async_copy(wk_any, wk_buf, kv_sem.at[0])
     v_copy = pltpu.make_async_copy(wv_any, wv_buf, kv_sem.at[1])
 
@@ -59,13 +63,12 @@
 
     gain = as_row(gain_ref)
     shift = as_row(shift_ref)
-    x_copy.wait()
     k_copy.start()
     v_copy.start()
-    for i in range(bands // 2):
-        q_copy(i).start()
+    q_copy(0).start()
 
     def norm_rows(i, carry):
+        x_copy(i).wait()
         at = pl.ds(pl.multiple_of(i * 16, 16), 16)
         vals = x_buf[at, :].astype(F32)
         mean = jnp.sum(vals, axis=-1, keepdims=True) * (1.0 / width)
@@ -75,6 +78,8 @@
         return carry
 
     lax.fori_loop(0, rows // 16, norm_rows, 0, unroll=2)
+    for i in range(1, bands // 2):
+        q_copy(i).start()
 
     perm = one_hot_rows(rows, batch)
     cos_t = cos_ref[...]
@@ -131,45 +136,55 @@
     def group(i, carry):
         for cp in cache_in(i):
             cp.wait()
-        for pr in range(per // 2):
+        s_shape = (heads, pair_rows, local)
+        o_shape = (heads, pair_rows, head_dim)
+
+        def rows_of(pr):
+            return pl.ds(pl.multiple_of(i * (per * steps) + pair_rows * pr, pair_rows), pair_rows)
+
+        def mask_of(pr):
             b0 = i * per + 2 * pr
-            rows_at = pl.ds(pl.multiple_of(i * (per * steps) + pair_rows * pr, pair_rows), pair_rows)
-            pos0 = pos_ref[b0]
-            pos1 = pos_ref[b0 + 1]
-            cur = jnp.where(row < steps, pos0, pos1) + step
+            cur = jnp.where(row < steps, pos_ref[b0], pos_ref[b0 + 1]) + step
             if slots & (slots - 1):
                 dist = lax.rem(lax.rem(cur - slot, slots) + slots, slots)
             else:
                 dist = (cur - slot) & (slots - 1)
-            old_ok = ((dist > step) & (dist <= cur))[None]
-            query = qkv[0:heads, rows_at, :].reshape(heads * pair_rows, head_dim).astype(BF16)
-            new_k = jnp.concatenate([qkv[heads, rows_at, :], pad], axis=0).astype(BF16)
-            new_v = jnp.concatenate([qkv[heads + 1, rows_at, :], pad], axis=0).astype(BF16)
-            shape = (heads, pair_rows, local)
-            score0 = lax.dot_general(query, k_buf[b0], nt, preferred_element_type=F32).reshape(shape)
-            score1 = lax.dot_general(query, k_buf[b0 + 1], nt, preferred_element_type=F32).reshape(shape)
-            score = jnp.where(old_ok, jnp.where((row < steps)[None], score0, score1) * scale, NEG_BIG)
-            shape = (heads, pair_rows, head_dim)
-            score_n = lax.dot_general(query, new_k, nt, preferred_element_type=F32).reshape(shape) * scale
-            score_n = jnp.where(new_ok, score_n, NEG_BIG)
+            return ((dist > step) & (dist <= cur))[None]
+
+        for pr in range(per // 2):
+            b0 = i * per + 2 * pr
+            query = qkv[0:heads, rows_of(pr), :].reshape(heads * pair_rows, head_dim).astype(BF16)
+            new_k = jnp.concatenate([qkv[heads, rows_of(pr), :], pad], axis=0).astype(BF16)
+            score0 = lax.dot_general(query, k_buf[b0], nt, preferred_element_type=F32).reshape(s_shape)
+            score1 = lax.dot_general(query, k_buf[b0 + 1], nt, preferred_element_type=F32).reshape(s_shape)
+            s_buf[pr] = jnp.where(mask_of(pr), jnp.where((row < steps)[None], score0, score1) * scale, NEG_BIG)
+            score_n = lax.dot_general(query, new_k, nt, preferred_element_type=F32).reshape(o_shape) * scale
+            n_buf[pr] = jnp.where(new_ok, score_n, NEG_BIG)
+        for pr in range(per // 2):
+            score = s_buf[pr]
+            score_n = n_buf[pr]
             top = jnp.max(jnp.maximum(score_n, functools.reduce(
                 jnp.maximum, [score[:, :, j:j + head_dim] for j in range(0, local, head_dim)])), axis=-1, keepdims=True)
-            wts = jnp.where(old_ok, jnp.exp(score - top), 0.0)
+            wts = jnp.where(mask_of(pr), jnp.exp(score - top), 0.0)
             wts_n = jnp.where(new_ok, jnp.exp(score_n - top), 0.0)
             total = jnp.sum(wts_n + sum(wts[:, :, j:j + head_dim] for j in range(0, local, head_dim)), axis=-1, keepdims=True)
-            wts = wts.reshape(heads * pair_rows, local).astype(BF16)
-            wts_n = wts_n.reshape(heads * pair_rows, head_dim).astype(BF16)
-            out0 = jnp.dot(wts, v_buf[b0], preferred_element_type=F32).reshape(shape)
-            out1 = jnp.dot(wts, v_buf[b0 + 1], preferred_element_type=F32).reshape(shape)
-            out_n = jnp.dot(wts_n, new_v, preferred_element_type=F32).reshape(shape)
-            out = jnp.where((n_row < steps)[None], out0, out1) + out_n
+            p_buf[pr, :, 0:local] = wts.reshape(heads * pair_rows, local).astype(BF16)
+            p_buf[pr, :, local:] = wts_n.reshape(heads * pair_rows, head_dim).astype(BF16)
             for core in range(2):
-                part_ref[core, 0:half, rows_at, :] = out[core * half:(core + 1) * half]
                 stat = jnp.zeros((pair_rows, head_dim), F32)
                 for h in range(half):
                     stat = jnp.where(lane == h, top[core * half + h], stat)
                     stat = jnp.where(lane == head_dim // 2 + h, total[core * half + h], stat)
-                part_ref[core, half, rows_at, :] = stat
+                part_ref[core, half, rows_of(pr), :] = stat
+        for pr in range(per // 2):
+            b0 = i * per + 2 * pr
+            new_v = jnp.concatenate([qkv[heads + 1, rows_of(pr), :], pad], axis=0).astype(BF16)
+            out0 = jnp.dot(p_buf[pr, :, 0:local], v_buf[b0], preferred_element_type=F32).reshape(o_shape)
+            out1 = jnp.dot(p_buf[pr, :, 0:local], v_buf[b0 + 1], preferred_element_type=F32).reshape(o_shape)
+            out_n = jnp.dot(p_buf[pr, :, local:], new_v, preferred_element_type=F32).reshape(o_shape)
+            out = jnp.where((n_row < steps)[None], out0, out1) + out_n
+            for core in range(2):
+                part_ref[core, 0:half, rows_of(pr), :] = out[core * half:(core + 1) * half]
         for b in range(per):
             lead = pos_ref[i * per + b] - first
             head_at = lax.rem(lead + slots, slots)
@@ -217,7 +232,7 @@
 
 def tail_kernel(part_ref, x_any, bo_ref, bpj_ref, gain_ref, shift_ref, bfc_ref, wo_any, wfc_any, wpj_any, y_ref,
                 w_buf, x_buf, pair_in, m_part, x_in, a_own, a_in, a_full, o_part, o_in, x1_all, hid,
-                g_own, g_in, g_full, p_part, p_in, y_all, bias_rows, w_sem, x_sem, send, recv, *, half, head_dim):
+                g_own, g_in, g_full, p_part, p_in, y_all, bias_rows, w_ext, w_sem, x_sem, send, recv, *, half, head_dim):
     steps, blk_b, cols = x_buf.shape
     blk = steps * blk_b
     n = 4
@@ -266,6 +281,10 @@
                                      w_sem.at[n + j]) for j in range(n)]
     pj_copy = [pltpu.make_async_copy(wpj_any.at[:, pl.ds(block_col(d), cols)], w_buf.at[k], w_sem.at[2 * n + k])
                for k, d in enumerate(order)]
+    hc = cols // 2
+    pj_copy[1] = pltpu.make_async_copy(wpj_any.at[:, pl.ds(pl.multiple_of(block_col(1) + hc, hc), hc)], w_buf.at[1, :, pl.ds(0, hc)],
+                                       w_sem.at[2 * n + 1])
+    ext_copy = pltpu.make_async_copy(wpj_any.at[:, pl.ds(block_col(1), hc)], w_ext, w_sem.at[3 * n])
     x_copy = pltpu.make_async_copy(x_any.at[:, pl.ds(pl.multiple_of(x * blk_b, blk_b), blk_b), pl.ds(my_col, cols)], x_buf, x_sem)
     x_copy.start()
     for d in order:
@@ -346,6 +365,7 @@
 
     ring_reduce(o_block, lambda d, rows: o_part.at[d, rows], o_in, along_y, fold_o)
     pj_copy[0].start()
+    ext_copy.start()
     x_copy.wait()
     x_own = x_buf[...].astype(F32).reshape(blk, cols) + bias_rows[0:1, pl.ds(my_col, cols)]
     hb = blk // 2
@@ -404,15 +424,23 @@
         if j < n - 1:
             pj_copy[j + 1].start()
     other_ff = pl.multiple_of((1 - c) * (ff // 2), ff // 2)
-    for j in range(n):
-        g_copy[j].wait_recv()
-        g_full[:, pl.ds(pl.multiple_of(other_ff + j * cols, cols), cols)] = g_in[j].astype(BF16)
 
     def p_block(d):
         k = order.index(d)
         pj_copy[k].wait()
-
-        p_part[d] = jnp.dot(g_full[...], w_buf[k], preferred_element_type=F32)
+        if k == 0:
+            own_rows, other_rows = pl.ds(own_ff, ff // 2), pl.ds(other_ff, ff // 2)
+            p_part[d] = jnp.dot(g_full[:, own_rows], w_buf[k, own_rows, :], preferred_element_type=F32)
+            for j in range(n):
+                g_copy[j].wait_recv()
+                g_full[:, pl.ds(pl.multiple_of(other_ff + j * cols, cols), cols)] = g_in[j].astype(BF16)
+            p_part[d] = p_part[d] + jnp.dot(g_full[:, other_rows], w_buf[k, other_rows, :], preferred_element_type=F32)
+        elif k == 1:
+            ext_copy.wait()
+            p_part[d, :, 0:hc] = jnp.dot(g_full[...], w_ext[...], preferred_element_type=F32)
+            p_part[d, :, hc:] = jnp.dot(g_full[...], w_buf[k, :, 0:hc], preferred_element_type=F32)
+        else:
+            p_part[d] = jnp.dot(g_full[...], w_buf[k], preferred_element_type=F32)
 
     def fold_p(d, rows, i):
         p_part[d, rows, :] = p_part[d, rows, :] + p_in[i]
@@ -502,6 +530,16 @@
         cp.wait_send()
 
 
+def copy_kernel(src, dst, buf, in_sem, out_sem):
+    for i in range(buf.shape[0]):
+        pltpu.make_async_copy(src.at[i], buf.at[i], in_sem.at[i]).start()
+    for i in range(buf.shape[0]):
+        pltpu.make_async_copy(src.at[i], buf.at[i], in_sem.at[i]).wait()
+        pltpu.make_async_copy(buf.at[i], dst.at[i], out_sem.at[i]).start()
+    for i in range(buf.shape[0]):
+        pltpu.make_async_copy(buf.at[i], dst.at[i], out_sem.at[i]).wait()
+
+
 def solution(mesh):
     n_sq = mesh.shape["sq"]
     n_y = mesh.shape["tp"]
@@ -530,12 +568,13 @@
         inv_freq = jnp.power(jnp.float32(ROPE_BASE), -2.0 * jnp.arange(half_dim, dtype=F32) / head_dim)
         inv_freq = jnp.concatenate([inv_freq, inv_freq])[None, None, :]
         sign = jnp.where(jnp.arange(head_dim) < half_dim, -1.0, 1.0).astype(F32)
-        cur = positions[None, :, None] + jnp.arange(steps, dtype=jnp.int32)[:, None, None]
+        shape = (steps, batch, head_dim)
+        cur = jnp.broadcast_to(positions[None, :, None], shape) + lax.broadcasted_iota(jnp.int32, shape, 0)
         angle = cur.astype(F32) * inv_freq
         cos_t = jnp.cos(angle).reshape(rows, head_dim)
         sin_t = (jnp.sin(angle) * sign).reshape(rows, head_dim)
 
-        per, bands = 4, 6
+        per, bands = 8, 6
         groups = batch // per
         smem = pl.BlockSpec(memory_space=pltpu.SMEM)
         part, k_new, v_new = pl.pallas_call(
@@ -555,7 +594,10 @@
                 pltpu.VMEM((heads + 2, rows, head_dim), F32),
                 pltpu.VMEM((batch, local, head_dim), BF16),
                 pltpu.VMEM((batch, local, head_dim), BF16),
-                pltpu.SemaphoreType.DMA,
+                pltpu.VMEM((per // 2, heads, 2 * steps, local), F32),
+                pltpu.VMEM((per // 2, heads, 2 * steps, head_dim), F32),
+                pltpu.VMEM((per // 2, heads * 2 * steps, local + head_dim), BF16),
+                pltpu.SemaphoreType.DMA((rows // 16,)),
                 pltpu.SemaphoreType.DMA((bands,)),
                 pltpu.SemaphoreType.DMA((2,)),
                 pltpu.SemaphoreType.DMA((2, groups)),
@@ -595,7 +637,8 @@
                 pltpu.VMEM((6, blk // 2, cols), F32),
                 pltpu.VMEM((4, 8, blk, cols), F32),
                 pltpu.VMEM((40, width), F32),
-                pltpu.SemaphoreType.DMA((12,)),
+                pltpu.VMEM((w_proj.shape[0], cols // 2), BF16),
+                pltpu.SemaphoreType.DMA((13,)),
                 pltpu.SemaphoreType.DMA,
                 pltpu.SemaphoreType.DMA((100,)),
                 pltpu.SemaphoreType.DMA((100,)),
@@ -603,6 +646,14 @@
             compiler_params=pltpu.CompilerParams(collective_id=0, has_side_effects=True, vmem_limit_bytes=VMEM_BYTES),
             name="tail",
         )(part, x_steps, b_o, b_proj, ln2_gain, ln2_bias, b_fc, w_o, w_fc, w_proj)
+        ys = pl.pallas_call(
+            copy_kernel,
+            out_shape=jax.ShapeDtypeStruct(ys.shape, ys.dtype),
+            in_specs=[hbm],
+            out_specs=hbm,
+            scratch_shapes=[pltpu.VMEM(ys.shape, ys.dtype), pltpu.SemaphoreType.DMA((steps,)), pltpu.SemaphoreType.DMA((steps,))],
+            name="ys_copy",
+        )(ys)
         return ys, k_new.reshape(key_buf.shape), v_new.reshape(val_buf.shape)
 
     return jax.shard_map(per_device, mesh=mesh, in_specs=in_specs, out_specs=out_specs, check_vma=False)

time: 98.6 us -> 93.9 us (0.952)
  local copies, waits for them, and re-layouts: 3.52 us -> 0.08 us
  Pallas kernels: 92.7 us -> 90.8 us
    pallas_call x1, Pallas kernels: 21.1 us -> 17.2 us  [per_device(): pl.pallas_call(functools.partial(front_kernel, batch=batch, heads=heads,...]
    unnamed x1 -> x0, local copies, waits for them, and re-layouts: 2.69 us -> none
    pallas_call x0 -> x1, Pallas kernels: none -> 2.2 us  [per_device(): pl.pallas_call(copy_kernel, out_shape=jax.ShapeDtypeStruct(ys.shape, ys.d...]
where the time goes in v4:
time: 93.9 us; the launch traced here: 93.5 us
  Pallas kernels  90.8 us (97%)
  other arithmetic  1.71 us (2%)
    pallas_call x1, Pallas kernels, per_device(): pl.pallas_call(functools.partial(tail_kernel, half=half, head_dim=head_di...  71.4 us
    pallas_call x1, Pallas kernels, per_device(): pl.pallas_call(functools.partial(front_kernel, batch=batch, heads=heads,...  17.2 us
    pallas_call x1, Pallas kernels, per_device(): pl.pallas_call(copy_kernel, out_shape=jax.ShapeDtypeStruct(ys.shape, ys.d...  2.2 us

profile of v4, /device:TPU:97, one launch (start us, length us, event | category | flops | bytes accessed | tf_op | source)
XLA Modules:
  0.0 93.5 jit_solution(7245554681508925236)
XLA Ops:
  0.6 0.1 compare_select_fusion
  0.7 0.7 add_convert_fusion
  1.4 0.1 convert_element_type.11
  1.5 1.0 %fusion = (f32[128,128]{1,0:T(8,128)}, f32[128,128]{1,0:T(8,128)}) fusion(f32[128]{0:T(128)S(1)} %get-tuple-element.14, f32[128]{0:T(128)S(1)} %get-tuple-element.15, f32[128]{0:T(128)S(1)} %convert_element_type.11), kind=kLoop, calls=%fused_computation.2 | loop fusion | flops 32768 | bytes 132608 | tf_op jit(solution)/shard_map/mul | solution.py:575
  2.4 17.2 %front.1 = (f32[2,7,128,128]{3,2,1,0:T(8,128)}, bf16[32,512,128]{2,1,0:T(8,128)(2,1)}, bf16[32,512,128]{2,1,0:T(8,128)(2,1)}) custom-call(s32[32]{0:T(128)} %pos_ref.1, bf16[128,6144]{1,0:T(8,128)(2,1)} %bitcast.9, bf16[6144,1536]{1,0:T(8,128)(2,1)} %wq_any.1, bf16[6144,128]{1,0:T(8,128)(2,1)} %wk_any.1, bf16[6144,128]{1,0:T(8,128)(2,1)} %wv_any.1, ...), custom_call_target="tpu_custom_call" | custom-call | tf_op jit(solution)/shard_map/front/pallas_call | solution.py:580
  19.7 71.4 %tail.1.src = bf16[4,32,6144]{2,1,0:T(8,128)(2,1)} custom-call(f32[2,7,128,128]{3,2,1,0:T(8,128)} %get-tuple-element.6.part_ref, bf16[4,32,6144]{2,1,0:T(8,128)(2,1)} %x_any.1, bf16[6144]{0:T(1024)(128)(2,1)} %bo_ref.1, bf16[6144]{0:T(1024)(128)(2,1)} %bpj_ref.1, bf16[6144]{0:T(1024)(128)(2,1)} %gain_ref.3, bf16[6144]{0:T(1024)(128)(2,1)} %shift_ref.3, ...), custom_call_target="tpu_custom_call" | custom-call | tf_op jit(solution)/shard_map/tail/pallas_call | solution.py:615
  91.1 2.2 %ys_copy.1 = bf16[4,32,6144]{2,1,0:T(8,128)(2,1)} custom-call(bf16[4,32,6144]{2,1,0:T(8,128)(2,1)} %tail.1.src), custom_call_target="tpu_custom_call" | custom-call | tf_op jit(solution)/shard_map/ys_copy/pallas_call | solution.py:649
  (1 shorter events, 0.0 us)

commit v5 on v4

--- a/solution.py
+++ b/solution.py
@@ -24,10 +24,11 @@
     return jnp.where(col == source, 1.0, 0.0).astype(BF16)
 
 
-def front_kernel(pos_ref, x_any, wq_any, wk_any, wv_any, gain_ref, shift_ref, bq_ref, bk_ref, bv_ref, cos_ref, sin_ref,
+def front_kernel(pos_ref, x_any, wq_any, wk_any, wv_any, gain_any, shift_any, bq_any, bk_any, bv_any, cos_any, sin_any,
                  kc_any, vc_any,
                  part_ref, kout_any, vout_any,
                  x_buf, hid, wq_buf, wk_buf, wv_buf, acc, qkv, k_buf, v_buf, s_buf, n_buf, p_buf,
+                 gain_ref, shift_ref, bq_ref, bk_ref, bv_ref, cos_ref, sin_ref, par_sem,
                  x_sem, wq_sem, kv_sem, c_sem, out_sem, *, batch, heads, head_dim, steps, per):
     rows, width = x_buf.shape
     n_q = heads * head_dim
@@ -43,7 +44,13 @@
         at = pl.ds(pl.multiple_of(i * 16, 16), 16)
         return pltpu.make_async_copy(x_any.at[at], x_buf.at[at], x_sem.at[i])
 
-    for i in range(rows // 16):
+    params = [pltpu.make_async_copy(src, dst, par_sem.at[i]) for i, (src, dst) in enumerate(
+        ((gain_any, gain_ref), (shift_any, shift_ref), (bq_any, bq_ref), (bk_any, bk_ref), (bv_any, bv_ref),
+         (cos_any, cos_ref), (sin_any, sin_ref)))]
+    x_copy(0).start()
+    for cp in params:
+        cp.start()
+    for i in range(1, rows // 16):
         x_copy(i).start()
     k_copy = pltpu.make_async_copy(wk_any, wk_buf, kv_sem.at[0])
     v_copy = pltpu.make_async_copy(wv_any, wv_buf, kv_sem.at[1])
@@ -61,11 +68,13 @@
         return (pltpu.make_async_copy(k_buf.at[at], kout_any.at[at], out_sem.at[0, i]),
                 pltpu.make_async_copy(v_buf.at[at], vout_any.at[at], out_sem.at[1, i]))
 
-    gain = as_row(gain_ref)
-    shift = as_row(shift_ref)
     k_copy.start()
     v_copy.start()
     q_copy(0).start()
+    for cp in params:
+        cp.wait()
+    gain = as_row(gain_ref)
+    shift = as_row(shift_ref)
 
     def norm_rows(i, carry):
         x_copy(i).wait()
@@ -230,9 +239,9 @@
     return outs, stat
 
 
-def tail_kernel(part_ref, x_any, bo_ref, bpj_ref, gain_ref, shift_ref, bfc_ref, wo_any, wfc_any, wpj_any, y_ref,
+def tail_kernel(part_any, x_any, bo_any, bpj_any, gain_any, shift_any, bfc_any, wo_any, wfc_any, wpj_any, y_ref,
                 w_buf, x_buf, pair_in, m_part, x_in, a_own, a_in, a_full, o_part, o_in, x1_all, hid,
-                g_own, g_in, g_full, p_part, p_in, y_all, bias_rows, w_ext, w_sem, x_sem, send, recv, *, half, head_dim):
+                g_own, g_in, g_full, p_part, p_in, y_all, bias_rows, w_ext, part_ref, bo_ref, bpj_ref, gain_ref, shift_ref, bfc_ref, par_sem, w_sem, x_sem, send, recv, *, half, head_dim):
     steps, blk_b, cols = x_buf.shape
     blk = steps * blk_b
     n = 4
@@ -286,15 +295,21 @@
                                        w_sem.at[2 * n + 1])
     ext_copy = pltpu.make_async_copy(wpj_any.at[:, pl.ds(block_col(1), hc)], w_ext, w_sem.at[3 * n])
     x_copy = pltpu.make_async_copy(x_any.at[:, pl.ds(pl.multiple_of(x * blk_b, blk_b), blk_b), pl.ds(my_col, cols)], x_buf, x_sem)
+    params = [pltpu.make_async_copy(src, dst, par_sem.at[i]) for i, (src, dst) in enumerate(
+        ((part_any, part_ref), (bo_any, bo_ref), (bpj_any, bpj_ref), (gain_any, gain_ref), (shift_any, shift_ref),
+         (bfc_any, bfc_ref)))]
+    for cp in params:
+        cp.start()
     x_copy.start()
     for d in order:
         wo_copy[d].start()
-    fc_copy[0].start()
 
     barrier = pltpu.get_barrier_semaphore()
     peers = [partner] + [along_x(d) for d in (1, 3)] + [along_y(d) for d in (1, 3)]
     for dev in peers:
         pl.semaphore_signal(barrier, inc=1, device_id=dev, device_id_type=MESH)
+    for cp in params:
+        cp.wait()
     for i, ref in enumerate((bo_ref, bpj_ref, bfc_ref, gain_ref, shift_ref)):
         bias_rows[8 * i:8 * i + 1, :] = as_row(ref)
     pl.semaphore_wait(barrier, len(peers))
@@ -322,6 +337,7 @@
     for d in order:
         at = pl.ds(pl.multiple_of(lax.rem(x + d, n) * blk, blk), blk)
         pairs[d] = push(part_ref.at[1 - c, :, at, :], pair_in.at[d], partner)
+    fc_copy[0].start()
     fc_copy[1].start()
 
     def pair_merge(d):
@@ -468,22 +484,18 @@
         for key, dev in (("xp", xp), ("xm", xm), ("yp", yp), ("ym", ym)):
             own[key, first_half] = relay(0, 0, dev, at=left if (key[1] == "p") == first_half else right)
     forward(0, 0)
-    own["xp", True].wait_recv()
-    r_xp = relay(3, 0, xp, at=left)
-    own["xm", True].wait_recv()
-    r_xm = relay(1, 0, xm, at=right)
-    own["yp", True].wait_recv()
-    r_yp = relay(0, 3, yp, at=left)
-    own["ym", True].wait_recv()
-    r_ym = relay(0, 1, ym, at=right)
-    own["xp", False].wait_recv()
-    a_yp, a_ym = relay(3, 0, yp, rows=lo), relay(3, 0, ym, rows=lo)
-    own["xm", False].wait_recv()
-    b_yp, b_ym = relay(1, 0, yp, rows=lo), relay(1, 0, ym, rows=lo)
-    own["yp", False].wait_recv()
-    a_xp, a_xm = relay(0, 3, xp, rows=hi), relay(0, 3, xm, rows=hi)
-    own["ym", False].wait_recv()
-    b_xp, b_xm = relay(0, 1, xp, rows=hi), relay(0, 1, xm, rows=hi)
+    step1 = (("xp", 3, 0, xp), ("xm", 1, 0, xm), ("yp", 0, 3, yp), ("ym", 0, 1, ym))
+    ring, turn = {}, {}
+    for first_half in (True, False):
+        for key, dx, dy, dev in step1:
+            own[key, first_half].wait_recv()
+            at = left if (key[1] == "p") == first_half else right
+            if first_half:
+                ring[key] = relay(dx, dy, dev, at=at)
+            rows = lo if dx else hi
+            for other, turn_dev in ((("yp", yp), ("ym", ym)) if dx else (("xp", xp), ("xm", xm))):
+                turn[key, other, at is left] = relay(dx, dy, turn_dev, rows, at)
+    r_xp, r_xm, r_yp, r_ym = ring["xp"], ring["xm"], ring["yp"], ring["ym"]
     for d in ((3, 0), (1, 0), (0, 3), (0, 1)):
         forward(*d)
     r_xp.wait_recv()
@@ -497,12 +509,16 @@
     forward(2, 0)
     forward(0, 2)
     late = []
-    for cp, dx, dy, dev, rows, at in ((a_yp, 3, 3, yp, lo, left), (a_ym, 3, 1, ym, lo, right),
-                                      (b_yp, 1, 3, yp, lo, left), (b_ym, 1, 1, ym, lo, right),
-                                      (a_xp, 3, 3, xp, hi, left), (a_xm, 1, 3, xm, hi, right),
-                                      (b_xp, 3, 1, xp, hi, left), (b_xm, 1, 1, xm, hi, right)):
-        cp.wait_recv()
-        late.append(relay(dx, dy, dev, rows, at))
+    for key, dx, dy, dev in step1:
+        rows = lo if dx else hi
+        for other, turn_dev in ((("yp", yp), ("ym", ym)) if dx else (("xp", xp), ("xm", xm))):
+            back = 3 if other[1] == "p" else 1
+            on_left = other[1] == "p"
+            turn[key, other, on_left].wait_recv()
+            late.append(relay(dx or back, dy or back, turn_dev, rows, left if on_left else right))
+    for key, dx, dy, dev in step1:
+        for other in (("yp", "ym") if dx else ("xp", "xm")):
+            turn[key, other, other[1] != "p"].wait_recv()
     for d in ((3, 3), (3, 1), (1, 3), (1, 1)):
         forward(*d)
     for cp, dx, dy, dev, rows, at in ((c_yp, 2, 3, yp, lo, left), (d_ym, 2, 1, ym, lo, right),
@@ -582,7 +598,7 @@
             out_shape=(jax.ShapeDtypeStruct((2, half + 1, rows, head_dim), F32),
                        jax.ShapeDtypeStruct((batch, local, head_dim), BF16),
                        jax.ShapeDtypeStruct((batch, local, head_dim), BF16)),
-            in_specs=[smem] + [hbm] * 4 + [vmem] * 7 + [hbm] * 2,
+            in_specs=[smem] + [hbm] * 13,
             out_specs=(vmem, hbm, hbm),
             scratch_shapes=[
                 pltpu.VMEM((rows, width), BF16),
@@ -597,6 +613,14 @@
                 pltpu.VMEM((per // 2, heads, 2 * steps, local), F32),
                 pltpu.VMEM((per // 2, heads, 2 * steps, head_dim), F32),
                 pltpu.VMEM((per // 2, heads * 2 * steps, local + head_dim), BF16),
+                pltpu.VMEM((width,), BF16),
+                pltpu.VMEM((width,), BF16),
+                pltpu.VMEM((heads * head_dim,), BF16),
+                pltpu.VMEM((head_dim,), BF16),
+                pltpu.VMEM((head_dim,), BF16),
+                pltpu.VMEM((rows, head_dim), F32),
+                pltpu.VMEM((rows, head_dim), F32),
+                pltpu.SemaphoreType.DMA((7,)),
                 pltpu.SemaphoreType.DMA((rows // 16,)),
                 pltpu.SemaphoreType.DMA((bands,)),
                 pltpu.SemaphoreType.DMA((2,)),
@@ -615,7 +639,7 @@
         ys = pl.pallas_call(
             functools.partial(tail_kernel, half=half, head_dim=head_dim),
             out_shape=jax.ShapeDtypeStruct((steps, batch, width), BF16),
-            in_specs=[vmem, hbm] + [vmem] * 5 + [hbm] * 3,
+            in_specs=[hbm] * 10,
             out_specs=vmem,
             scratch_shapes=[
                 pltpu.VMEM((5, width, cols), BF16),
@@ -638,10 +662,17 @@
                 pltpu.VMEM((4, 8, blk, cols), F32),
                 pltpu.VMEM((40, width), F32),
                 pltpu.VMEM((w_proj.shape[0], cols // 2), BF16),
+                pltpu.VMEM(part.shape, F32),
+                pltpu.VMEM((width,), BF16),
+                pltpu.VMEM((width,), BF16),
+                pltpu.VMEM((width,), BF16),
+                pltpu.VMEM((width,), BF16),
+                pltpu.VMEM(b_fc.shape, BF16),
+                pltpu.SemaphoreType.DMA((6,)),
                 pltpu.SemaphoreType.DMA((13,)),
                 pltpu.SemaphoreType.DMA,
-                pltpu.SemaphoreType.DMA((100,)),
-                pltpu.SemaphoreType.DMA((100,)),
+                pltpu.SemaphoreType.DMA((112,)),
+                pltpu.SemaphoreType.DMA((112,)),
             ],
             compiler_params=pltpu.CompilerParams(collective_id=0, has_side_effects=True, vmem_limit_bytes=VMEM_BYTES),
             name="tail",

time: 93.9 us -> 95.1 us (1.013)
  Pallas kernels: 90.8 us -> 92.3 us
where the time goes in v5:
time: 95.1 us; the launch traced here: 94.9 us
  Pallas kernels  92.3 us (97%)
  other arithmetic  1.71 us (2%)
    pallas_call x1, Pallas kernels, per_device(): pl.pallas_call(functools.partial(tail_kernel, half=half, head_dim=head_di...  72 us
    pallas_call x1, Pallas kernels, per_device(): pl.pallas_call(functools.partial(front_kernel, batch=batch, heads=heads,...  18 us
    pallas_call x1, Pallas kernels, per_device(): pl.pallas_call(copy_kernel, out_shape=jax.ShapeDtypeStruct(ys.shape, ys.d...  2.2 us

profile of v5, /device:TPU:97, one launch (start us, length us, event | category | flops | bytes accessed | tf_op | source)
XLA Modules:
  0.0 94.9 jit_solution(15083296610048572624)
XLA Ops:
  0.6 0.1 compare_select_fusion
  0.7 0.7 add_convert_fusion
  1.4 0.1 convert_element_type.11
  1.5 1.0 %fusion = (f32[128,128]{1,0:T(8,128)}, f32[128,128]{1,0:T(8,128)}) fusion(f32[128]{0:T(128)S(1)} %get-tuple-element.14, f32[128]{0:T(128)S(1)} %get-tuple-element.15, f32[128]{0:T(128)S(1)} %convert_element_type.11), kind=kLoop, calls=%fused_computation.2 | loop fusion | flops 32768 | bytes 132608 | tf_op jit(solution)/shard_map/mul | solution.py:591
  2.4 18.0 %front.1 = (f32[2,7,128,128]{3,2,1,0:T(8,128)}, bf16[32,512,128]{2,1,0:T(8,128)(2,1)}, bf16[32,512,128]{2,1,0:T(8,128)(2,1)}) custom-call(s32[32]{0:T(128)} %pos_ref.1, bf16[128,6144]{1,0:T(8,128)(2,1)} %bitcast.9, bf16[6144,1536]{1,0:T(8,128)(2,1)} %wq_any.1, bf16[6144,128]{1,0:T(8,128)(2,1)} %wk_any.1, bf16[6144,128]{1,0:T(8,128)(2,1)} %wv_any.1, ...), custom_call_target="tpu_custom_call" | custom-call | tf_op jit(solution)/shard_map/front/pallas_call | solution.py:596
  20.5 72.0 %tail.1.src = bf16[4,32,6144]{2,1,0:T(8,128)(2,1)} custom-call(f32[2,7,128,128]{3,2,1,0:T(8,128)} %get-tuple-element.6.part_any, bf16[4,32,6144]{2,1,0:T(8,128)(2,1)} %x_any.1, bf16[6144]{0:T(1024)(128)(2,1)} %bo_any.1, bf16[6144]{0:T(1024)(128)(2,1)} %bpj_any.1, bf16[6144]{0:T(1024)(128)(2,1)} %gain_any.3, bf16[6144]{0:T(1024)(128)(2,1)} %shift_any.3, ...), custom_call_target="tpu_custom_call" | custom-call | tf_op jit(solution)/shard_map/tail/pallas_call | solution.py:639
  92.5 2.2 %ys_copy.1 = bf16[4,32,6144]{2,1,0:T(8,128)(2,1)} custom-call(bf16[4,32,6144]{2,1,0:T(8,128)(2,1)} %tail.1.src), custom_call_target="tpu_custom_call" | custom-call | tf_op jit(solution)/shard_map/ys_copy/pallas_call | solution.py:680
  (1 shorter events, 0.0 us)
